TPU v7x, 32 devices: a whole 2x2x4 slice. The times are simulated.
32 devices in a mesh: grp: 4 (over x, core), slab: 8 (over z, y).
Axes of the slice: x: 2, y: 2, z: 4, core: 2. Of those that a mesh axis runs over, the one named last changes fastest.
Arguments:
- velocity: float32 [3, 8, 256, 256], P(None, 'slab', 'grp'), may hold values from -2.5 to 2.5
- fields: bfloat16 [8, 3, 8, 256, 256], P('grp', None, 'slab'), may hold values from -8 to 8
- noise: float32 [8, 3], P('grp'), may hold values from -4 to 4
Outputs:
- new_velocity: float32 [3, 8, 256, 256], P(None, 'slab', 'grp')
- new_fields: bfloat16 [8, 3, 8, 256, 256], P('grp', None, 'slab')
All inputs are finite; a program needn't handle non-finite values.
Results may differ from a plain program's by a relative error of at most 0.0004.
Values may be sent and summed in bfloat16 or wider, within the bound.
No kernel may reach another device: no remote copies, remote signals or barrier semaphores. Data moves between devices by JAX's collectives and lax.ppermute only.
A program may use at most 64 MiB of HBM per device.

v0:
```python
import math

import jax
import jax.numpy as jnp
import numpy as np
from jax import lax
from jax.experimental import pallas as pl
from jax.experimental.pallas import tpu as pltpu
from jax.sharding import PartitionSpec as P

TIME_STEP = 0.05
RELAX_TIME = 0.1
STRETCH_MAX = 36.0
POLY_MODULUS = 2.0
VISCOSITY = 0.2
NOISE_SCALE = math.sqrt(TIME_STEP / RELAX_TIME)
TENSOR_PAIRS = ((0, 0), (1, 1), (2, 2), (0, 1), (0, 2), (1, 2))


def extended(block, sides, width):
    for axis, dim in sides:
        count = lax.axis_size(axis)
        forward = [(i, i + 1) for i in range(count - 1)]
        forward.append((count - 1, 0))
        backward = [(target, source) for source, target in forward]
        low = lax.ppermute(
            lax.slice_in_dim(block, block.shape[dim] - width, None, axis=dim), axis, forward
        )
        high = lax.ppermute(lax.slice_in_dim(block, 0, width, axis=dim), axis, backward)
        block = jnp.concatenate([low, block, high], axis=dim)
    return block


def pair_slot(first_axis, second_axis):
    return TENSOR_PAIRS.index((min(first_axis, second_axis), max(first_axis, second_axis)))


def centred(values, axis):
    return (jnp.roll(values, -1, axis) - jnp.roll(values, 1, axis)) * 0.5


def stack_gradient(parts):
    return jnp.stack(
        [parts[direction][component] for component in range(3) for direction in range(3)]
    )


def pair_products(conform):
    return jnp.stack(
        [jnp.sum(conform[:, first] * conform[:, second], axis=0) for first, second in TENSOR_PAIRS]
    )


def stretch_factor(mean_square):
    return 1.0 / (1.0 - mean_square / STRETCH_MAX)


def poly_stress(sums, stretch, field_total):
    identity = jnp.array([1.0, 1.0, 1.0, 0.0, 0.0, 0.0], jnp.float32)[:, None, None, None]
    return POLY_MODULUS * (stretch * sums / field_total - identity)


def dft_tables(length):
    counter = jnp.arange(length, dtype=jnp.int32)
    phase = counter[:, None] * counter[None, :] % length
    angle = phase.astype(jnp.float32) * (2.0 * math.pi / length)
    return (jnp.cos(angle), jnp.sin(angle))


def along_axis(values, table, axis):
    letters = "abcdef"[: values.ndim]
    result = letters[:axis] + "k" + letters[axis + 1 :]
    return jnp.einsum(
        letters + "," + letters[axis] + "k->" + result,
        values,
        table,
        precision=lax.Precision.HIGHEST,
    )


def complex_pass(stacked, axis, forward):
    cosine, sine_table = dft_tables(stacked.shape[axis])
    cos_terms = along_axis(stacked, cosine, axis)
    sin_terms = along_axis(stacked, sine_table, axis)
    if forward:
        return jnp.stack([cos_terms[0] + sin_terms[1], cos_terms[1] - sin_terms[0]])
    return jnp.stack([cos_terms[0] - sin_terms[1], cos_terms[1] + sin_terms[0]])


def wavenumber(indices, length):
    signed = jnp.where(indices < length // 2, indices, indices - length)
    return signed.astype(jnp.float32) * (2.0 * math.pi / length)


def shards(velocity, fields, noise):
    grp_count = lax.axis_size("grp")
    grp_index = lax.axis_index("grp")
    slab_count = lax.axis_size("slab")
    slab_index = lax.axis_index("slab")
    field_total = fields.shape[0] * grp_count
    row_count = velocity.shape[2]
    row_start = grp_index * row_count
    width_y = velocity.shape[3]
    rimmed = extended(velocity, (("grp", 2), ("slab", 1)), 1)
    along_x = (rimmed[:, 1:-1, 2:, :] - rimmed[:, 1:-1, :-2, :]) * 0.5
    along_y = centred(velocity, 3)
    along_z = (rimmed[:, 2:, 1:-1, :] - rimmed[:, :-2, 1:-1, :]) * 0.5
    grad_rows = stack_gradient((along_x, along_y, along_z))
    grad_plane, vel_plane = (
        lax.all_gather(grad_rows, "grp", axis=2, tiled=True),
        lax.all_gather(velocity, "grp", axis=2, tiled=True),
    )
    field_rim = extended(fields, (("slab", 2),), 1)
    conform = fields.astype(jnp.float32)
    field_dz = (
        field_rim[:, :, 2:].astype(jnp.float32) - field_rim[:, :, :-2].astype(jnp.float32)
    ) * 0.5
    summed = lax.psum(pair_products(conform), "grp")
    stretch = stretch_factor((summed[0] + summed[1] + summed[2]) / field_total)
    stress_plane = poly_stress(summed, stretch, field_total)
    wrapped = jnp.concatenate(
        [stress_plane[:, :, -1:], stress_plane, stress_plane[:, :, :1]], axis=2
    )
    stress_rows = lax.dynamic_slice_in_dim(wrapped, row_start, row_count + 2, 2)
    stress_pad = extended(stress_rows, (("slab", 1),), 1)
    updated = []
    for component in range(3):
        member = conform[:, component]
        advect = (
            vel_plane[0] * centred(member, 2)
            + vel_plane[1] * centred(member, 3)
            + vel_plane[2] * field_dz[:, component]
        )
        stretching = sum(
            (
                grad_plane[3 * component + direction] * conform[:, direction]
                for direction in range(3)
            )
        )
        drift = stretching - advect - stretch * member / (2.0 * RELAX_TIME)
        updated.append(
            member + TIME_STEP * drift + NOISE_SCALE * noise[:, component][:, None, None, None]
        )
    new_fields = jnp.stack(updated, axis=1).astype(jnp.bfloat16)
    forcing = []
    for component in range(3):
        convect = sum(
            (velocity[direction] * grad_rows[3 * component + direction] for direction in range(3))
        )
        slot_x = pair_slot(component, 0)
        slot_y = pair_slot(component, 1)
        slot_z = pair_slot(component, 2)
        divergence = (stress_pad[slot_x, 1:-1, 2:, :] - stress_pad[slot_x, 1:-1, :-2, :]) * 0.5
        divergence = divergence + centred(stress_pad[slot_y, 1:-1, 1:-1, :], 2)
        divergence = (
            divergence + (stress_pad[slot_z, 2:, 1:-1, :] - stress_pad[slot_z, :-2, 1:-1, :]) * 0.5
        )
        forcing.append(velocity[component] + TIME_STEP * (divergence - convect))
    forcing = jnp.stack(forcing)
    cosine_y, sine_y = dft_tables(width_y)
    flat = forcing.reshape(-1, width_y)
    real_part = jnp.dot(flat, cosine_y, precision=lax.Precision.HIGHEST).reshape(forcing.shape)
    imag_part = -jnp.dot(flat, sine_y, precision=lax.Precision.HIGHEST).reshape(forcing.shape)
    spectrum = jnp.stack([real_part, imag_part])
    spectrum = lax.all_to_all(spectrum, "grp", split_axis=4, concat_axis=3, tiled=True)
    spectrum = complex_pass(spectrum, 3, True)
    spectrum = lax.all_to_all(spectrum, "slab", split_axis=3, concat_axis=2, tiled=True)
    spectrum = complex_pass(spectrum, 2, True)
    total_z = spectrum.shape[2]
    cols_x = spectrum.shape[3]
    cols_y = spectrum.shape[4]
    total_x = cols_x * slab_count
    total_y = cols_y * grp_count
    wave_z = wavenumber(jnp.arange(total_z, dtype=jnp.int32), total_z)[:, None, None]
    wave_x = wavenumber(slab_index * cols_x + jnp.arange(cols_x, dtype=jnp.int32), total_x)[
        None, :, None
    ]
    wave_y = wavenumber(grp_index * cols_y + jnp.arange(cols_y, dtype=jnp.int32), total_y)[
        None, None, :
    ]
    waves = (wave_x, wave_y, wave_z)
    square = wave_x * wave_x + wave_y * wave_y + wave_z * wave_z
    safe_square = jnp.where(square > 0, square, 1.0)
    projected = (
        wave_x * spectrum[:, 0] + wave_y * spectrum[:, 1] + wave_z * spectrum[:, 2]
    ) / safe_square
    damping = 1.0 + VISCOSITY * TIME_STEP * square
    solved = jnp.stack(
        [
            (spectrum[:, component] - waves[component] * projected) / damping
            for component in range(3)
        ],
        axis=1,
    )
    solved = complex_pass(solved, 2, False)
    solved = lax.all_to_all(solved, "slab", split_axis=2, concat_axis=3, tiled=True)
    solved = complex_pass(solved, 3, False)
    solved = lax.all_to_all(solved, "grp", split_axis=3, concat_axis=4, tiled=True)
    flat_real = solved[0].reshape(-1, width_y)
    flat_imag = solved[1].reshape(-1, width_y)
    combined = jnp.dot(flat_real, cosine_y, precision=lax.Precision.HIGHEST) - jnp.dot(
        flat_imag, sine_y, precision=lax.Precision.HIGHEST
    )
    new_velocity = combined.reshape(velocity.shape) / (width_y * total_x * total_z)
    return (new_velocity, new_fields)


ROW_TILE = 16


def real_basis(length):
    half = length // 2
    cell = np.arange(length)
    wave = np.arange(half)
    angle = (cell[:, None] * wave[None, :] % length) * (2.0 * math.pi / length)
    sine = np.sin(angle)
    sine[:, 0] = np.where(cell % 2 == 0, 1.0, -1.0)
    return np.concatenate([np.cos(angle), sine], axis=1)


def split_table(table):
    high = jnp.asarray(table.astype(jnp.bfloat16))
    low = jnp.asarray((table - table.astype(jnp.bfloat16).astype(np.float64)).astype(jnp.bfloat16))
    return high, low


def split_value(value):
    high = value.astype(jnp.bfloat16)
    return high, (value - high.astype(jnp.float32)).astype(jnp.bfloat16)


def dot_split(left, right, dims):
    def one(a, b):
        return lax.dot_general(a, b, (dims, ((), ())), preferred_element_type=jnp.float32)

    return one(left[0], right[0]) + (one(left[0], right[1]) + one(left[1], right[0]))


def row_index(shape):
    return lax.broadcasted_iota(jnp.int32, shape, 0)


def lane_index(shape):
    return lax.broadcasted_iota(jnp.int32, shape, 1)


def row_after(block, last):
    rows = block.shape[0]
    moved = pltpu.roll(block, rows - 1, 0)
    return jnp.where(row_index(block.shape) == rows - 1, last, moved)


def row_before(block, first):
    moved = pltpu.roll(block, 1, 0)
    return jnp.where(row_index(block.shape) == 0, first, moved)


def lane_difference(block):
    lanes = block.shape[1]
    return pltpu.roll(block, lanes - 1, 1) - pltpu.roll(block, 1, 1)


def whole(array):
    rank = len(array.shape)
    return pl.BlockSpec(array.shape, lambda *_: (0,) * rank)


def run_kernel(body, outs, args, scalars=(), scratch=(), cost=None):
    in_specs = [pl.BlockSpec(memory_space=pltpu.SMEM) for _ in scalars]
    in_specs += [whole(a) for a in args]
    return pl.pallas_call(
        body,
        out_shape=outs,
        grid=(1,),
        in_specs=in_specs,
        out_specs=jax.tree.map(whole, outs),
        scratch_shapes=scratch,
        cost_estimate=cost,
        name=body.__name__ if hasattr(body, "__name__") else None,
    )(*scalars, *args)


def pack_rows(fields, grp_index, groups):
    members, dims, size_x, size_y = fields.shape
    rows = size_x // groups
    planes = members * dims
    rim = -(-2 * planes // ROW_TILE) * ROW_TILE
    shape = jax.ShapeDtypeStruct((planes * rows + rim, size_y), fields.dtype)

    def pack(index, source, *targets):
        for shift, target in enumerate(targets):
            block = (index[0] + shift) % groups
            start = pl.multiple_of(block * rows, rows)
            above = pl.multiple_of((block + groups - 1) % groups * rows + rows - ROW_TILE, ROW_TILE)
            below = pl.multiple_of((block + 1) % groups * rows, rows)
            edge = jnp.zeros((rim, size_y), jnp.float32)
            place = row_index((rim, size_y))
            for member in range(members):
                for dim in range(dims):
                    plane = member * dims + dim
                    target[plane * rows : (plane + 1) * rows, :] = source[
                        member, dim, pl.ds(start, rows), :
                    ]
                    top = source[member, dim, pl.ds(above, ROW_TILE), :].astype(jnp.float32)
                    bottom = source[member, dim, pl.ds(below, ROW_TILE), :].astype(jnp.float32)
                    slot = dim * 2 * members + member * 2
                    edge = jnp.where(place == slot, top[ROW_TILE - 1 :], edge)
                    edge = jnp.where(place == slot + 1, bottom[:1], edge)
            target[planes * rows :, :] = edge.astype(fields.dtype)

    return run_kernel(pack, [shape] * groups, [fields], [grp_index])


def force_rows(blocks, motion, above, below, table, members, field_total):
    rows, size_y = motion.shape[1:]
    planes = 3 * members

    def stress_of(sums):
        stretch = stretch_factor((sums[0] + sums[1] + sums[2]) / field_total)
        return stretch, [
            POLY_MODULUS * (stretch * sums[slot] / field_total - (1.0 if first == second else 0.0))
            for slot, (first, second) in enumerate(TENSOR_PAIRS)
        ]

    def force(*refs):
        parts = refs[: len(blocks)]
        flow, top, bottom, table_high, table_low, out, stretch_out, stress, stack = refs[
            len(blocks) :
        ]
        for start in range(0, rows, ROW_TILE):
            sums = [None] * 6
            for part in parts:
                for member in range(members):
                    vector = [
                        part[
                            (member * 3 + dim) * rows + start : (member * 3 + dim) * rows
                            + start
                            + ROW_TILE,
                            :,
                        ].astype(jnp.float32)
                        for dim in range(3)
                    ]
                    for slot, (first, second) in enumerate(TENSOR_PAIRS):
                        term = vector[first] * vector[second]
                        sums[slot] = term if sums[slot] is None else sums[slot] + term
            stretch, values = stress_of(sums)
            stretch_out[start : start + ROW_TILE, :] = stretch
            for slot in range(6):
                stress[slot, start : start + ROW_TILE, :] = values[slot]
        sums = [None] * 6
        for part in parts:
            edge = part[planes * rows :, :].astype(jnp.float32)
            vector = [edge[dim * 2 * members : (dim + 1) * 2 * members] for dim in range(3)]
            for slot, (first, second) in enumerate(TENSOR_PAIRS):
                term = vector[first] * vector[second]
                sums[slot] = term if sums[slot] is None else sums[slot] + term
        sums = [
            sum(value[2 * member : 2 * member + 2] for member in range(members)) for value in sums
        ]
        edges = stress_of(sums)[1]
        half = 0.5 * TIME_STEP
        place = {0: 0, 1: 1, 2: 4}
        for component in range(3):
            slot_x = pair_slot(component, 0)
            slot_y = pair_slot(component, 1)
            slot_z = pair_slot(component, 2)
            value = stress[slot_x]
            total = row_after(value, edges[slot_x][1:2]) - row_before(value, edges[slot_x][0:1])
            total = total + lane_difference(stress[slot_y])
            own = flow[component]
            total = total - flow[0] * (
                row_after(own, bottom[component]) - row_before(own, top[component])
            )
            total = total - flow[1] * lane_difference(own)
            total = total - (2.0 * flow[2]) * flow[3 + component]
            spot = place[component]
            stack[spot * rows : (spot + 1) * rows, :] = own + half * total
            spot = spot + (2 if component < 2 else 1)
            stack[spot * rows : (spot + 1) * rows, :] = half * stress[slot_z]
        out[...] = dot_split(
            (table_high[...], table_low[...]), split_value(stack[...]), ((1,), (1,))
        )

    return run_kernel(
        force,
        [
            jax.ShapeDtypeStruct((size_y, 6 * rows), jnp.float32),
            jax.ShapeDtypeStruct((rows, size_y), jnp.float32),
        ],
        [*blocks, motion, above, below, *table],
        scratch=[
            pltpu.VMEM((6, rows, size_y), jnp.float32),
            pltpu.VMEM((6 * rows, size_y), jnp.float32),
        ],
    )


def solve_pencil(pencil, device_index, table, groups, total_z, size_y):
    block = pencil.shape[1]
    pairs = block // 2
    rows = pencil.shape[2] // 6
    size_x = rows * groups
    half_x = size_x // 2
    half_z = total_z // 2
    basis_z = real_basis(total_z)
    lines = total_z * block
    step_x = 2.0 * math.pi / size_x
    step_y = 2.0 * math.pi / size_y
    step_z = 2.0 * math.pi / total_z

    def join(first, second, lane):
        return jnp.where(lane < rows, first, pltpu.roll(second, rows, 1))

    def solve(index, source, table_high, table_low, out, stack, result):
        lane = lane_index((block, 2 * rows))
        for pair in range(groups // 2):
            both = []
            for side in range(2):
                group = 2 * pair + side
                tiles = [
                    [
                        source[group * total_z + z, :, t * 2 * rows : (t + 1) * 2 * rows]
                        for t in range(3)
                    ]
                    for z in range(total_z)
                ]
                both.append(
                    [
                        (
                            tiles[z][0] + tiles[(z + 1) % total_z][1] - tiles[z - 1][1],
                            tiles[z][2]
                            + pltpu.roll(tiles[(z + 1) % total_z][2] - tiles[z - 1][2], rows, 1),
                        )
                        for z in range(total_z)
                    ]
                )
            columns = slice(pair * 2 * rows, (pair + 1) * 2 * rows)
            for z in range(total_z):
                (first, third), (first_b, third_b) = both[0][z], both[1][z]
                line = z * block
                stack[line : line + block, columns] = join(first, first_b, lane)
                stack[lines + line : lines + line + block, columns] = jnp.where(
                    lane < rows, pltpu.roll(first, rows, 1), first_b
                )
                stack[2 * lines + line : 2 * lines + line + block, columns] = join(
                    third, third_b, lane
                )
        table_x = (table_high[...], table_low[...])
        result[...] = dot_split(split_value(stack[...]), table_x, ((1,), (0,)))

        shape = (block, size_x)
        lane = lane_index(shape)
        row = row_index(shape)
        wave = (lane % half_x).astype(jnp.float32) * step_x
        nyquist_x = jnp.where(lane == half_x, math.pi, 0.0)
        swap_x = jnp.where(lane < half_x, wave, -wave)
        square_x = wave * wave + nyquist_x * nyquist_x
        weight_x = jnp.where(lane % half_x == 0, 1.0, 2.0)
        number = index[0] * pairs + row % pairs
        wave = number.astype(jnp.float32) * step_y
        nyquist_y = jnp.where((number == 0) & (row >= pairs), math.pi, 0.0)
        swap_y = jnp.where(row < pairs, wave, -wave)
        square_y = wave * wave + nyquist_y * nyquist_y
        weight_y = jnp.where(number == 0, 1.0, 2.0)
        square_xy = square_x + square_y
        scale = weight_x * weight_y / (size_x * size_y * total_z)

        def along_x(value):
            return swap_x * pltpu.roll(value, half_x, 1)

        def along_y(value):
            return swap_y * pltpu.roll(value, pairs, 0)

        waves = []
        for component in range(3):
            planes = [
                result[component * lines + z * block : component * lines + (z + 1) * block, :]
                for z in range(total_z)
            ]
            waves.append(
                [
                    sum(float(basis_z[z, k]) * planes[z] for z in range(total_z))
                    for k in range(total_z)
                ]
            )

        def partner(k):
            if k % half_z == 0:
                return k, 0.0
            return (k + half_z, step_z * k) if k < half_z else (k - half_z, -step_z * (k - half_z))

        potential = []
        factors = []
        extra = []
        for k in range(total_z):
            wave_z = step_z * (k % half_z) if k != half_z else math.pi
            square = square_xy + wave_z * wave_z
            safe = jnp.where(square > 0, square, 1.0)
            other, factor = partner(k)
            total = along_x(waves[0][k]) + along_y(waves[1][k])
            if factor != 0.0:
                total = total + factor * waves[2][other]
            potential.append(total / safe)
            nyquist = nyquist_x * waves[0][k] + nyquist_y * waves[1][k]
            if k == half_z:
                nyquist = nyquist + math.pi * waves[2][k]
            extra.append(nyquist / safe)
            weight_z = 1.0 if k % half_z == 0 else 2.0
            factors.append(scale * weight_z / (1.0 + VISCOSITY * TIME_STEP * square))
        solved = [[], [], []]
        for k in range(total_z):
            other, factor = partner(k)
            solved[0].append(
                factors[k] * (waves[0][k] + along_x(potential[k]) - nyquist_x * extra[k])
            )
            solved[1].append(
                factors[k] * (waves[1][k] + along_y(potential[k]) - nyquist_y * extra[k])
            )
            value = waves[2][k]
            if factor != 0.0:
                value = value + factor * potential[other]
            if k == half_z:
                value = value - math.pi * extra[k]
            solved[2].append(factors[k] * value)
        for component in range(3):
            for z in range(total_z):
                line = component * lines + z * block
                stack[line : line + block, :] = sum(
                    float(basis_z[z, k]) * solved[component][k] for k in range(total_z)
                )
        result[...] = dot_split(split_value(stack[...]), table_x, ((1,), (1,)))
        lane = lane_index((block, 2 * rows))
        for group in range(groups):
            columns = slice(group // 2 * 2 * rows, (group // 2 + 1) * 2 * rows)
            for z in range(total_z):
                line = z * block
                first, second, third = [
                    result[c * lines + line : c * lines + line + block, columns] for c in range(3)
                ]
                if group % 2 == 0:
                    front = join(first, second, lane)
                else:
                    front = jnp.where(lane < rows, pltpu.roll(first, rows, 1), second)
                    third = pltpu.roll(third, rows, 1)
                out[group * total_z + z, :, : 2 * rows] = front
                out[group * total_z + z, :, 2 * rows :] = third

    return run_kernel(
        solve,
        jax.ShapeDtypeStruct((groups * total_z, block, 4 * rows), jnp.float32),
        [pencil, *table],
        [device_index],
        scratch=[
            pltpu.VMEM((3 * lines, size_x), jnp.float32),
            pltpu.VMEM((3 * lines, size_x), jnp.float32),
        ],
    )


def rows_from_waves(spectra, table, rows):
    size_y = table[0].shape[1]

    def synthesise(source, table_high, table_low, out):
        turned = source[...].T[: 3 * rows]
        value = dot_split(
            split_value(turned), (table_high[...], table_low[...]), ((1,), (0,))
        )
        for component in range(3):
            out[component, 0] = value[component * rows : (component + 1) * rows]

    return run_kernel(
        synthesise,
        jax.ShapeDtypeStruct((3, 1, rows, size_y), jnp.float32),
        [spectra, *table],
    )


def advance_fields(fields, paired, passed, motions, stretches, noise, spots, sign):
    members, dims, size_x, size_y = fields.shape
    count = len(motions)
    rows = size_x // count
    steps = size_x // ROW_TILE

    def advance(spot, signs, kick, *refs):
        own, near, far = refs[:3]
        flows = refs[3 : 3 + count]
        factors = refs[3 + count : 3 + 2 * count]
        out, plane, factor = refs[3 + 2 * count :]
        for number in range(count):
            start = pl.multiple_of(spot[number] * rows, rows)
            for slot in range(6):
                plane[slot, pl.ds(start, rows), :] = flows[number][slot]
            factor[pl.ds(start, rows), :] = factors[number][...]
        side = signs[0].astype(jnp.float32)
        half = 0.5 * TIME_STEP

        def step(number, carry):
            start = pl.multiple_of(number * ROW_TILE, ROW_TILE)
            before = pl.multiple_of((number + steps - 1) % steps * ROW_TILE, ROW_TILE)
            after = pl.multiple_of((number + 1) % steps * ROW_TILE, ROW_TILE)
            here = pl.ds(start, ROW_TILE)
            speed = [half * plane[c, here, :] for c in range(3)]
            slope = []
            for c in range(3):
                first = half * plane[c, pl.ds(before, ROW_TILE), :][ROW_TILE - 1 :]
                last = half * plane[c, pl.ds(after, ROW_TILE), :][:1]
                slope.append(
                    (
                        row_after(speed[c], last) - row_before(speed[c], first),
                        lane_difference(speed[c]),
                        TIME_STEP * plane[3 + c, here, :],
                    )
                )
            keep = 1.0 - (TIME_STEP / (2.0 * RELAX_TIME)) * factor[here, :]
            lift = side * speed[2]
            for member in range(members):
                vector = [own[member, c, here, :].astype(jnp.float32) for c in range(3)]
                for c in range(3):
                    first = own[member, c, pl.ds(before, ROW_TILE), :].astype(jnp.float32)
                    last = own[member, c, pl.ds(after, ROW_TILE), :].astype(jnp.float32)
                    value = vector[c]
                    rise = near[member, c, here, :].astype(jnp.float32) - far[
                        member, c, here, :
                    ].astype(jnp.float32)
                    total = keep * value + NOISE_SCALE * kick[member, c]
                    for j in range(3):
                        total = total + slope[c][j] * vector[j]
                    total = total - speed[0] * (
                        row_after(value, last[:1]) - row_before(value, first[ROW_TILE - 1 :])
                    )
                    total = total - speed[1] * lane_difference(value)
                    total = total - lift * rise
                    out[member, c, here, :] = total.astype(jnp.bfloat16)
            return carry

        lax.fori_loop(0, steps, step, 0)

    return run_kernel(
        advance,
        jax.ShapeDtypeStruct(fields.shape, jnp.bfloat16),
        [fields, paired, passed, *motions, *stretches],
        [spots, sign, noise],
        scratch=[
            pltpu.VMEM((6, size_x, size_y), jnp.float32),
            pltpu.VMEM((size_x, size_y), jnp.float32),
        ],
        cost=pl.CostEstimate(flops=60000000, bytes_accessed=5000000, transcendentals=0),
    )


def shifted(value, axis, step):
    count = lax.axis_size(axis)
    return lax.ppermute(value, axis, [(i, (i + step) % count) for i in range(count)])


def flipped(value, axis, bit):
    count = lax.axis_size(axis)
    return lax.ppermute(value, axis, [(i, i ^ bit) for i in range(count)])


def spread(value, axis):
    bit = lax.axis_size(axis) // 2
    found = [(0, value)]
    while bit:
        found += [(offset ^ bit, flipped(held, axis, bit)) for offset, held in found]
        bit //= 2
    return found


def pencil_shards(velocity, fields, noise):
    groups = lax.axis_size("grp")
    slabs = lax.axis_size("slab")
    grp_index = lax.axis_index("grp")
    slab_index = lax.axis_index("slab")
    members, dims, _, size_x, size_y = fields.shape
    rows = velocity.shape[2]
    devices = groups * slabs
    block = size_y // devices
    half_block = block // 2
    order = np.concatenate(
        [
            np.concatenate([np.arange(half_block), size_y // 2 + np.arange(half_block)])
            + device * half_block
            for device in range(devices)
        ]
    )
    table_y = split_table(np.ascontiguousarray(real_basis(size_y).T[order]))
    table_x = split_table(real_basis(size_x))

    flow = velocity[:, 0]
    above = shifted(flow[:, -1:], "grp", 1)
    below = shifted(flow[:, :1], "grp", -1)
    lower = shifted(flow, "slab", 1)
    upper = shifted(flow, "slab", -1)
    plane = fields[:, :, 0]
    blocks = pack_rows(plane, grp_index.reshape(1), groups)
    blocks = [blocks[0]] + [shifted(blocks[d], "grp", d) for d in range(1, groups)]
    paired = flipped(plane, "slab", 1)
    passed = lax.ppermute(
        paired, "slab", [(i, (i + (-2 if i % 2 else 2)) % slabs) for i in range(slabs)]
    )
    motion = jnp.concatenate([flow, (upper - lower) * 0.5], axis=0)
    motions = spread(motion, "grp")
    spectra, stretch = force_rows(
        blocks, motion, above, below, table_y, members, members * groups
    )
    stretches = spread(stretch, "grp")
    pencil = lax.all_to_all(
        spectra.reshape(devices, block, 6 * rows),
        ("grp", "slab"),
        split_axis=0,
        concat_axis=0,
        tiled=True,
    )
    device_index = (grp_index * slabs + slab_index).reshape(1)
    solved = solve_pencil(pencil, device_index, table_x, groups, slabs, size_y)
    spots = jnp.stack([grp_index ^ offset for offset, _ in motions])
    sign = (1 - 2 * (slab_index % 2)).reshape(1)
    new_fields = advance_fields(
        plane,
        paired,
        passed,
        [held for _, held in motions],
        [held for _, held in stretches],
        noise,
        spots,
        sign,
    )
    solved = lax.all_to_all(
        solved, ("grp", "slab"), split_axis=0, concat_axis=0, tiled=True
    )
    new_velocity = rows_from_waves(solved.reshape(size_y, 4 * rows), table_y, rows)
    return (new_velocity, new_fields[:, :, None])


def pencil_fits(mesh, velocity, fields):
    groups, slabs = mesh.shape["grp"], mesh.shape["slab"]
    size_z, size_x, size_y = velocity.shape[1:]
    return (
        size_z == slabs
        and slabs % 2 == 0
        and groups >= 2
        and groups & (groups - 1) == 0
        and size_y % (2 * groups * slabs) == 0
        and size_x % (groups * ROW_TILE) == 0
        and (2 * size_x // groups) % 128 == 0
        and fields.shape[0] % groups == 0
    )


def solution(mesh):
    def step(velocity, fields, noise):
        body = pencil_shards if pencil_fits(mesh, velocity, fields) else shards
        return jax.shard_map(
            body,
            mesh=mesh,
            in_specs=(
                P(None, "slab", "grp", None),
                P("grp", None, "slab", None, None),
                P("grp", None),
            ),
            out_specs=(P(None, "slab", "grp", None), P("grp", None, "slab", None, None)),
            check_vma=False,
        )(velocity, fields, noise)

    return step
```

profile of v0, /device:TPU:0, one launch (start us, length us, event | category | flops | bytes accessed | tf_op | source)
XLA Modules:
  0.0 88.4 jit_solution(15499257895098174480)
XLA Ops:
  0.6 6.1 %collective-permute-start.3 = (f32[3,64,256]{2,1,0:T(8,128)}, f32[3,64,256]{2,1,0:T(8,128)S(1)}, u32[]{:S(2)}, u32[]{:S(2)}) collective-permute-start(f32[3,64,256]{2,1,0:T(8,128)} %bitcast.19), channel_id=1, source_target_pairs={{0,7},{1,0},{2,1},{3,2},{4,3},{5,4},{6,5},{7,6},{8,15},{9,8},{10,9... | collective-permute-start | bytes 589832 | tf_op jit(solution)/shard_map/ppermute | solution.py:653
  6.7 0.0 collective-permute-start.4
  6.7 0.0 collective-permute-start.7
  6.7 0.0 copy-start.8
  6.7 2.2 %pack.1 = (bf16[400,256]{1,0:T(8,128)(2,1)}, bf16[400,256]{1,0:T(8,128)(2,1)}, bf16[400,256]{1,0:T(8,128)(2,1)}, bf16[400,256]{1,0:T(8,128)(2,1)}) custom-call(s32[1]{0:T(128)} %bitcast.1.index, bf16[2,3,256,256]{3,2,1,0:T(8,128)(2,1)} %bitcast.14), custom_call_target="tpu_custom_call" | custom-call | tf_op jit(solution)/shard_map/pack/pallas_call | solution.py:271
  8.9 0.0 collective-permute-start
  8.9 1.5 %collective-permute-start.1 = (bf16[400,256]{1,0:T(8,128)(2,1)}, bf16[400,256]{1,0:T(8,128)(2,1)S(1)}, u32[]{:S(2)}, u32[]{:S(2)}) collective-permute-start(bf16[400,256]{1,0:T(8,128)(2,1)} %get-tuple-element.10), channel_id=1, source_target_pairs={{0,16},{8,24},{16,0},{24,8},{1,17},{9,25},{17,1},{25,9},{2,18},{10... | collective-permute-start | bytes 614408 | tf_op jit(solution)/shard_map/ppermute | solution.py:653
  10.4 0.0 copy-done.8
  10.4 0.8 collective-permute-done.3
  11.2 0.7 collective-permute-start.2
  11.9 4.2 %collective-permute-done.4 = f32[3,64,256]{2,1,0:T(8,128)S(1)} collective-permute-done((f32[3,64,256]{2,1,0:T(8,128)}, f32[3,64,256]{2,1,0:T(8,128)S(1)}, u32[]{:S(2)}, u32[]{:S(2)}) %collective-permute-start.4) | collective-permute-done | bytes 196640 | tf_op jit(solution)/shard_map/ppermute | solution.py:653
  16.1 0.0 collective-permute-start.5
  16.1 4.2 %collective-permute-done.5.refs_5_ = f32[3,1,256]{2,1,0:T(1,128)S(1)} collective-permute-done((f32[3,1,256]{2,1,0:T(1,128)S(1)}, f32[3,1,256]{2,1,0:T(1,128)S(1)}, u32[]{:S(2)}, u32[]{:S(2)}) %collective-permute-start.5) | collective-permute-done | bytes 3104 | tf_op jit(solution)/shard_map/ppermute | solution.py:653
  20.4 0.0 collective-permute-start.6
  20.4 0.8 pad_maximum_fusion.refs_4_.refs_3_
  21.1 0.0 copy-done.14
  21.1 0.6 collective-permute-done.6.refs_6_
  21.7 0.0 copy-start.15
  21.7 0.0 collective-permute-done.refs_1_
  21.7 0.0 collective-permute-done.1.refs_2_
  21.7 0.0 copy-start.10
  21.7 0.0 collective-permute-done.2.refs_3_
  21.7 0.0 copy-start.11
  21.7 0.5 copy-done.15
  22.3 0.1 copy-done.9
  22.4 0.1 copy-done.10
  22.5 0.0 copy-done.11
  22.5 3.0 %force.1 = (f32[256,384]{1,0:T(8,128)}, f32[64,256]{1,0:T(8,128)}) custom-call(bf16[400,256]{1,0:T(8,128)(2,1)} %get-tuple-element.8.refs_0_, bf16[400,256]{1,0:T(8,128)(2,1)} %copy-done.9, bf16[400,256]{1,0:T(8,128)(2,1)} %copy-done.10, bf16[400,256]{1,0:T(8,128)(2,1)} %copy-done.11, f32[6,64,256]{2,1,0:T(8,128)} %pad_maximum_fusion.refs_4_.refs_3_, ...), custom_call_target="tpu_custom_call" | custom-call | tf_op jit(solution)/shard_map/force/pallas_call | solution.py:271
  25.6 7.1 %all-to-all-start = ((f32[32,8,384]{2,1,0:T(8,128)}), f32[32,8,384]{2,1,0:T(8,128)S(1)}, u32[]{:S(2)}, u32[]{:S(2)}) async-start(f32[32,8,384]{2,1,0:T(8,128)} %bitcast.18), calls=%async_computation | async-start | bytes 786432 | tf_op jit(solution)/shard_map/all_to_all | solution.py:708
  32.7 0.0 copy-done
  32.7 1.8 %collective-permute-start.9 = (f32[6,64,256]{2,1,0:T(8,128)S(1)}, f32[6,64,256]{2,1,0:T(8,128)S(1)}, u32[]{:S(2)}, u32[]{:S(2)}) collective-permute-start(f32[6,64,256]{2,1,0:T(8,128)S(1)} %copy-done), channel_id=1, source_target_pairs={{0,16},{8,24},{16,0},{24,8},{1,17},{9,25},{17,1},{25,9},{2,18},{10... | collective-permute-start | bytes 1179656 | tf_op jit(solution)/shard_map/ppermute | solution.py:658
  34.5 0.0 collective-permute-done.7.refs_1_
  34.5 1.5 %collective-permute-start.8 = (bf16[2,3,256,256]{3,2,1,0:T(8,128)(2,1)S(1)}, bf16[2,3,256,256]{3,2,1,0:T(8,128)(2,1)S(1)}, u32[]{:S(2)}, u32[]{:S(2)}) collective-permute-start(bf16[2,3,256,256]{3,2,1,0:T(8,128)(2,1)S(1)} %collective-permute-done.7.refs_1_), channel_id=1, source_target_pairs={{0,2},{1,7},{2,4},{3,1},{4,6},{5,3},{6,0},{7,5},{8,10},{9,15},{10,... | collective-permute-start | bytes 2359304 | tf_op jit(solution)/shard_map/ppermute | solution.py:699
  36.0 24.9 %all-to-all-done.source = f32[32,8,384]{2,1,0:T(8,128)S(1)} async-done(((f32[32,8,384]{2,1,0:T(8,128)}), f32[32,8,384]{2,1,0:T(8,128)S(1)}, u32[]{:S(2)}, u32[]{:S(2)}) %all-to-all-start) | async-done | bytes 393248 | tf_op jit(solution)/shard_map/all_to_all | solution.py:708
  60.9 0.7 copy-done.1
  61.7 2.6 %solve.1 = f32[32,8,256]{2,1,0:T(8,128)} custom-call(s32[1]{0:T(128)} %bitcast.index, f32[32,8,384]{2,1,0:T(8,128)} %copy-done.1, bf16[256,256]{1,0:T(8,128)(2,1)} %constant.38.clone.table_high, bf16[256,256]{1,0:T(8,128)(2,1)} %constant.39.clone.table_low), custom_call_target="tpu_custom_call" | custom-call | tf_op jit(solution)/shard_map/solve/pallas_call | solution.py:271
  64.3 4.4 %all-to-all-start.1 = ((f32[32,8,256]{2,1,0:T(8,128)}), f32[32,8,256]{2,1,0:T(8,128)S(1)}, u32[]{:S(2)}, u32[]{:S(2)}) async-start(f32[32,8,256]{2,1,0:T(8,128)} %solve.1), calls=%async_computation.1 | async-start | bytes 524288 | tf_op jit(solution)/shard_map/all_to_all | solution.py:729
  68.7 0.3 collective-permute-start.10
  69.0 0.0 collective-permute-done.9.refs_4_
  69.0 0.3 collective-permute-start.11
  69.3 0.0 copy-done.12
  69.3 1.8 %collective-permute-start.12 = (f32[64,256]{1,0:T(8,128)S(1)}, f32[64,256]{1,0:T(8,128)S(1)}, u32[]{:S(2)}, u32[]{:S(2)}) collective-permute-start(f32[64,256]{1,0:T(8,128)S(1)} %copy-done.12), channel_id=1, source_target_pairs={{0,16},{8,24},{16,0},{24,8},{1,17},{9,25},{17,1},{25,9},{2,18},{10... | collective-permute-start | bytes 196616 | tf_op jit(solution)/shard_map/ppermute | solution.py:658
  71.1 0.0 collective-permute-start.13
  71.1 3.8 %collective-permute-done.12.refs_8_ = f32[64,256]{1,0:T(8,128)S(1)} collective-permute-done((f32[64,256]{1,0:T(8,128)S(1)}, f32[64,256]{1,0:T(8,128)S(1)}, u32[]{:S(2)}, u32[]{:S(2)}) %collective-permute-start.12) | collective-permute-done | bytes 65568 | tf_op jit(solution)/shard_map/ppermute | solution.py:658
  74.8 0.0 collective-permute-start.14
  74.8 0.7 pad_add_fusion.spot
  75.5 3.7 %all-to-all-done.1 = f32[32,8,256]{2,1,0:T(8,128)S(1)} async-done(((f32[32,8,256]{2,1,0:T(8,128)}), f32[32,8,256]{2,1,0:T(8,128)S(1)}, u32[]{:S(2)}, u32[]{:S(2)}) %all-to-all-start.1) | async-done | bytes 262176 | tf_op jit(solution)/shard_map/all_to_all | solution.py:729
  79.1 0.7 copy-done.2
  79.9 2.0 %synthesise.1 = f32[3,1,64,256]{3,2,1,0:T(8,128)} custom-call(f32[256,256]{1,0:T(8,128)} %bitcast.16, bf16[256,256]{1,0:T(8,128)(2,1)} %constant.36.clone.refs_7_.table_high, bf16[256,256]{1,0:T(8,128)(2,1)} %constant.37.clone.refs_8_.table_low), custom_call_target="tpu_custom_call" | custom-call | tf_op jit(solution)/shard_map/synthesise/pallas_call | solution.py:271
  81.9 0.0 copy-done.13
  81.9 0.0 collective-permute-done.13.refs_9_
  81.9 0.0 collective-permute-done.14.refs_10_
  81.9 0.0 collective-permute-done.10.refs_5_
  81.9 0.0 copy-start.6
  81.9 0.0 collective-permute-done.11.refs_6_
  81.9 0.0 copy-start.7
  81.9 0.0 collective-permute-done.8.refs_2_
  81.9 0.0 copy-start.4
  81.9 0.0 copy-done.3
  81.9 0.0 copy-done.5
  82.0 0.7 copy-done.6
  82.7 0.1 copy-done.7
  82.8 0.3 copy-done.4
  83.0 5.4 %advance.1 = bf16[2,3,256,256]{3,2,1,0:T(8,128)(2,1)} custom-call(s32[4]{0:T(128)} %pad_add_fusion.spot, s32[1]{0:T(128)} %bitcast.9.signs, f32[2,3]{1,0:T(2,128)} %kick.1, bf16[2,3,256,256]{3,2,1,0:T(8,128)(2,1)} %bitcast.15, bf16[2,3,256,256]{3,2,1,0:T(8,128)(2,1)} %copy-done.3, bf16[2,3,256,256]{3,2,1,0:T(8,128)(2,1)} %copy-done.4, ...), custom_call_target="tpu_custom_call" | custom-call | flops 60000000 | bytes 5000000 | tf_op jit(solution)/shard_map/advance/pallas_call | solution.py:271
  (11 shorter events, 0.0 us)
Async XLA Ops:
  0.6 10.6 %collective-permute-start.3 = (f32[3,64,256]{2,1,0:T(8,128)}, f32[3,64,256]{2,1,0:T(8,128)S(1)}, u32[]{:S(2)}, u32[]{:S(2)}) collective-permute-start(f32[3,64,256]{2,1,0:T(8,128)} %bitcast.19), channel_id=1, source_target_pairs={{0,7},{1,0},{2,1},{3,2},{4,3},{5,4},{6,5},{7,6},{8,15},{9,8},{10,9... | collective-permute-start | bytes 589832 | tf_op jit(solution)/shard_map/ppermute | solution.py:653
  6.7 9.4 %collective-permute-start.4 = (f32[3,64,256]{2,1,0:T(8,128)}, f32[3,64,256]{2,1,0:T(8,128)S(1)}, u32[]{:S(2)}, u32[]{:S(2)}) collective-permute-start(f32[3,64,256]{2,1,0:T(8,128)} %bitcast.20), channel_id=1, source_target_pairs={{0,1},{1,2},{2,3},{3,4},{4,5},{5,6},{6,7},{7,0},{8,9},{9,10},{10,1... | collective-permute-start | bytes 589832 | tf_op jit(solution)/shard_map/ppermute | solution.py:653
  6.7 27.8 %collective-permute-start.7 = (bf16[2,3,256,256]{3,2,1,0:T(8,128)(2,1)}, bf16[2,3,256,256]{3,2,1,0:T(8,128)(2,1)S(1)}, u32[]{:S(2)}, u32[]{:S(2)}) collective-permute-start(bf16[2,3,256,256]{3,2,1,0:T(8,128)(2,1)} %bitcast.13), channel_id=1, source_target_pairs={{0,1},{1,0},{2,3},{3,2},{4,5},{5,4},{6,7},{7,6},{8,9},{9,8},{10,11... | collective-permute-start | bytes 2359304 | tf_op jit(solution)/shard_map/ppermute | solution.py:658
  6.7 3.7 %copy-start.8 = (f32[3,1,64,256]{3,2,1,0:T(8,128)S(1)}, f32[3,1,64,256]{3,2,1,0:T(8,128)}, u32[]{:S(2)}) copy-start(f32[3,1,64,256]{3,2,1,0:T(8,128)} %param.7) | copy-start | bytes 589828
  8.9 12.8 %collective-permute-start = (bf16[400,256]{1,0:T(8,128)(2,1)}, bf16[400,256]{1,0:T(8,128)(2,1)S(1)}, u32[]{:S(2)}, u32[]{:S(2)}) collective-permute-start(bf16[400,256]{1,0:T(8,128)(2,1)} %get-tuple-element.9), channel_id=1, source_target_pairs={{0,8},{8,16},{16,24},{24,0},{1,9},{9,17},{17,25},{25,1},{2,10},{10... | collective-permute-start | bytes 614408 | tf_op jit(solution)/shard_map/ppermute | solution.py:653
  8.9 12.8 %collective-permute-start.1 = (bf16[400,256]{1,0:T(8,128)(2,1)}, bf16[400,256]{1,0:T(8,128)(2,1)S(1)}, u32[]{:S(2)}, u32[]{:S(2)}) collective-permute-start(bf16[400,256]{1,0:T(8,128)(2,1)} %get-tuple-element.10), channel_id=1, source_target_pairs={{0,16},{8,24},{16,0},{24,8},{1,17},{9,25},{17,1},{25,9},{2,18},{10... | collective-permute-start | bytes 614408 | tf_op jit(solution)/shard_map/ppermute | solution.py:653
  11.2 10.5 %collective-permute-start.2 = (bf16[400,256]{1,0:T(8,128)(2,1)}, bf16[400,256]{1,0:T(8,128)(2,1)S(1)}, u32[]{:S(2)}, u32[]{:S(2)}) collective-permute-start(bf16[400,256]{1,0:T(8,128)(2,1)} %get-tuple-element.11), channel_id=1, source_target_pairs={{0,24},{8,0},{16,8},{24,16},{1,25},{9,1},{17,9},{25,17},{2,26},{10... | collective-permute-start | bytes 614408 | tf_op jit(solution)/shard_map/ppermute | solution.py:653
  16.1 4.3 %collective-permute-start.5 = (f32[3,1,256]{2,1,0:T(1,128)S(1)}, f32[3,1,256]{2,1,0:T(1,128)S(1)}, u32[]{:S(2)}, u32[]{:S(2)}) collective-permute-start(f32[3,1,256]{2,1,0:T(1,128)S(1)} %get-tuple-element.17), channel_id=1, source_target_pairs={{0,8},{8,16},{16,24},{24,0},{1,9},{9,17},{17,25},{25,1},{2,10},{10... | collective-permute-start | bytes 9224 | tf_op jit(solution)/shard_map/ppermute | solution.py:653
  20.4 0.8 copy-start.14
  20.4 1.3 %collective-permute-start.6 = (f32[3,1,256]{2,1,0:T(1,128)S(1)}, f32[3,1,256]{2,1,0:T(1,128)S(1)}, u32[]{:S(2)}, u32[]{:S(2)}) collective-permute-start(f32[3,1,256]{2,1,0:T(1,128)S(1)} %get-tuple-element.16), channel_id=1, source_target_pairs={{0,24},{8,0},{16,8},{24,16},{1,25},{9,1},{17,9},{25,17},{2,26},{10... | collective-permute-start | bytes 9224 | tf_op jit(solution)/shard_map/ppermute | solution.py:653
  21.7 0.6 copy-start.15
  21.7 0.7 copy-start.9
  21.7 0.8 copy-start.10
  21.7 0.8 copy-start.11
  25.6 7.1 %copy-start = (f32[6,64,256]{2,1,0:T(8,128)S(1)}, f32[6,64,256]{2,1,0:T(8,128)}, u32[]{:S(2)}) copy-start(f32[6,64,256]{2,1,0:T(8,128)} %pad_maximum_fusion.refs_4_.refs_3_) | copy-start | bytes 1179652
  25.6 35.4 %all-to-all-start = ((f32[32,8,384]{2,1,0:T(8,128)}), f32[32,8,384]{2,1,0:T(8,128)S(1)}, u32[]{:S(2)}, u32[]{:S(2)}) async-start(f32[32,8,384]{2,1,0:T(8,128)} %bitcast.18), calls=%async_computation | async-start | bytes 786432 | tf_op jit(solution)/shard_map/all_to_all | solution.py:708
  32.7 36.3 %collective-permute-start.9 = (f32[6,64,256]{2,1,0:T(8,128)S(1)}, f32[6,64,256]{2,1,0:T(8,128)S(1)}, u32[]{:S(2)}, u32[]{:S(2)}) collective-permute-start(f32[6,64,256]{2,1,0:T(8,128)S(1)} %copy-done), channel_id=1, source_target_pairs={{0,16},{8,24},{16,0},{24,8},{1,17},{9,25},{17,1},{25,9},{2,18},{10... | collective-permute-start | bytes 1179656 | tf_op jit(solution)/shard_map/ppermute | solution.py:658
  34.5 47.4 %copy-start.3 = (bf16[2,3,256,256]{3,2,1,0:T(8,128)(2,1)}, bf16[2,3,256,256]{3,2,1,0:T(8,128)(2,1)S(1)}, u32[]{:S(2)}) copy-start(bf16[2,3,256,256]{3,2,1,0:T(8,128)(2,1)S(1)} %collective-permute-done.7.refs_1_) | copy-start | bytes 2359300
  34.5 47.4 %collective-permute-start.8 = (bf16[2,3,256,256]{3,2,1,0:T(8,128)(2,1)S(1)}, bf16[2,3,256,256]{3,2,1,0:T(8,128)(2,1)S(1)}, u32[]{:S(2)}, u32[]{:S(2)}) collective-permute-start(bf16[2,3,256,256]{3,2,1,0:T(8,128)(2,1)S(1)} %collective-permute-done.7.refs_1_), channel_id=1, source_target_pairs={{0,2},{1,7},{2,4},{3,1},{4,6},{5,3},{6,0},{7,5},{8,10},{9,15},{10,... | collective-permute-start | bytes 2359304 | tf_op jit(solution)/shard_map/ppermute | solution.py:699
  60.9 0.7 copy-start.1
  64.3 5.0 %copy-start.12 = (f32[64,256]{1,0:T(8,128)S(1)}, f32[64,256]{1,0:T(8,128)}, u32[]{:S(2)}) copy-start(f32[64,256]{1,0:T(8,128)} %get-tuple-element.13.refs_7_) | copy-start | bytes 196612
  64.3 14.8 %all-to-all-start.1 = ((f32[32,8,256]{2,1,0:T(8,128)}), f32[32,8,256]{2,1,0:T(8,128)S(1)}, u32[]{:S(2)}, u32[]{:S(2)}) async-start(f32[32,8,256]{2,1,0:T(8,128)} %solve.1), calls=%async_computation.1 | async-start | bytes 524288 | tf_op jit(solution)/shard_map/all_to_all | solution.py:729
  68.7 13.2 %collective-permute-start.10 = (f32[6,64,256]{2,1,0:T(8,128)S(1)}, f32[6,64,256]{2,1,0:T(8,128)S(1)}, u32[]{:S(2)}, u32[]{:S(2)}) collective-permute-start(f32[6,64,256]{2,1,0:T(8,128)S(1)} %copy-done), channel_id=1, source_target_pairs={{0,8},{8,0},{16,24},{24,16},{1,9},{9,1},{17,25},{25,17},{2,10},{10... | collective-permute-start | bytes 1179656 | tf_op jit(solution)/shard_map/ppermute | solution.py:658
  69.0 12.9 %copy-start.5 = (f32[6,64,256]{2,1,0:T(8,128)}, f32[6,64,256]{2,1,0:T(8,128)S(1)}, u32[]{:S(2)}) copy-start(f32[6,64,256]{2,1,0:T(8,128)S(1)} %collective-permute-done.9.refs_4_) | copy-start | bytes 1179652
  69.0 12.9 %collective-permute-start.11 = (f32[6,64,256]{2,1,0:T(8,128)S(1)}, f32[6,64,256]{2,1,0:T(8,128)S(1)}, u32[]{:S(2)}, u32[]{:S(2)}) collective-permute-start(f32[6,64,256]{2,1,0:T(8,128)S(1)} %collective-permute-done.9.refs_4_), channel_id=1, source_target_pairs={{0,8},{8,0},{16,24},{24,16},{1,9},{9,1},{17,25},{25,17},{2,10},{10... | collective-permute-start | bytes 1179656 | tf_op jit(solution)/shard_map/ppermute | solution.py:658
  69.3 5.5 %collective-permute-start.12 = (f32[64,256]{1,0:T(8,128)S(1)}, f32[64,256]{1,0:T(8,128)S(1)}, u32[]{:S(2)}, u32[]{:S(2)}) collective-permute-start(f32[64,256]{1,0:T(8,128)S(1)} %copy-done.12), channel_id=1, source_target_pairs={{0,16},{8,24},{16,0},{24,8},{1,17},{9,25},{17,1},{25,9},{2,18},{10... | collective-permute-start | bytes 196616 | tf_op jit(solution)/shard_map/ppermute | solution.py:658
  71.1 10.8 %collective-permute-start.13 = (f32[64,256]{1,0:T(8,128)S(1)}, f32[64,256]{1,0:T(8,128)}, u32[]{:S(2)}, u32[]{:S(2)}) collective-permute-start(f32[64,256]{1,0:T(8,128)S(1)} %copy-done.12), channel_id=1, source_target_pairs={{0,8},{8,0},{16,24},{24,16},{1,9},{9,1},{17,25},{25,17},{2,10},{10... | collective-permute-start | bytes 196616 | tf_op jit(solution)/shard_map/ppermute | solution.py:658
  74.8 7.0 %copy-start.13 = (f32[64,256]{1,0:T(8,128)}, f32[64,256]{1,0:T(8,128)S(1)}, u32[]{:S(2)}) copy-start(f32[64,256]{1,0:T(8,128)S(1)} %collective-permute-done.12.refs_8_) | copy-start | bytes 196612
  74.8 7.0 %collective-permute-start.14 = (f32[64,256]{1,0:T(8,128)S(1)}, f32[64,256]{1,0:T(8,128)}, u32[]{:S(2)}, u32[]{:S(2)}) collective-permute-start(f32[64,256]{1,0:T(8,128)S(1)} %collective-permute-done.12.refs_8_), channel_id=1, source_target_pairs={{0,8},{8,0},{16,24},{24,16},{1,9},{9,1},{17,25},{25,17},{2,10},{10... | collective-permute-start | bytes 196616 | tf_op jit(solution)/shard_map/ppermute | solution.py:658
  79.1 0.7 copy-start.2
  81.9 0.8 copy-start.6
  81.9 0.9 copy-start.7
  81.9 1.1 %copy-start.4 = (bf16[2,3,256,256]{3,2,1,0:T(8,128)(2,1)}, bf16[2,3,256,256]{3,2,1,0:T(8,128)(2,1)S(1)}, u32[]{:S(2)}) copy-start(bf16[2,3,256,256]{3,2,1,0:T(8,128)(2,1)S(1)} %collective-permute-done.8.refs_2_) | copy-start | bytes 2359300
where the time goes:
time: 88.8 us; the launch traced here: 88.4 us
  waiting for transfers between devices  42.1 us (47%)
  starting transfers between devices  25.5 us (29%)
  Pallas kernels  15.3 us (17%)
  local copies, waits for them, and re-layouts  3.37 us (4%)
  other arithmetic  1.45 us (2%)
    all_to_all x1, waiting for transfers between devices, pencil_shards(): lax.all_to_all(spectra.reshape(devices, block, 6 * rows), ('grp', 'slab')...  24.9 us
    pallas_call x5, Pallas kernels, run_kernel(): pl.pallas_call(body, out_shape=outs, grid=(1,), in_specs=in_specs, out_sp...  15.3 us
    ppermute x7, waiting for transfers between devices, shifted(): lax.ppermute(value, axis, [(i, (i + step) % count) for i in range(count)])  9.73 us
    ppermute x7, starting transfers between devices, shifted(): lax.ppermute(value, axis, [(i, (i + step) % count) for i in range(count)])  8.33 us
    all_to_all x1, starting transfers between devices, pencil_shards(): lax.all_to_all(spectra.reshape(devices, block, 6 * rows), ('grp', 'slab')...  7.11 us
    all_to_all x1, starting transfers between devices, pencil_shards(): lax.all_to_all(solved, ('grp', 'slab'), split_axis=0, concat_axis=0, tile...  4.36 us
    ppermute x7, starting transfers between devices, flipped(): return lax.ppermute(value, axis, [(i, i ^ bit) for i in range(count)])  4.18 us
    ppermute x7, waiting for transfers between devices, flipped(): return lax.ppermute(value, axis, [(i, i ^ bit) for i in range(count)])  3.78 us
  transfers between devices with their start and end apart: 17, of which 7 were waited for; matrix products, arithmetic and copies ran while one was open for 2% of the time, Pallas kernels for 11%

commit v1 on v0

--- a/solution.py
+++ b/solution.py
@@ -206,6 +206,7 @@
 
 
 ROW_TILE = 16
+END_ROWS = 8
 
 
 def real_basis(length):
@@ -218,10 +219,12 @@
     return np.concatenate([np.cos(angle), sine], axis=1)
 
 
-def split_table(table):
-    high = jnp.asarray(table.astype(jnp.bfloat16))
-    low = jnp.asarray((table - table.astype(jnp.bfloat16).astype(np.float64)).astype(jnp.bfloat16))
-    return high, low
+def split_tables(*tables):
+    parts = []
+    for table in tables:
+        high = table.astype(jnp.bfloat16)
+        parts += [high, (table - high.astype(np.float64)).astype(jnp.bfloat16)]
+    return jnp.asarray(np.stack(parts))
 
 
 def split_value(value):
@@ -260,60 +263,128 @@
     return pltpu.roll(block, lanes - 1, 1) - pltpu.roll(block, 1, 1)
 
 
-def whole(array):
-    rank = len(array.shape)
-    return pl.BlockSpec(array.shape, lambda *_: (0,) * rank)
-
-
-def run_kernel(body, outs, args, scalars=(), scratch=(), cost=None):
+def run_kernel(body, outs, args, scalars=(), scratch=(), flops=0, far=()):
+    leaves = list(args) + jax.tree.leaves(outs)
+    leaves += [leaf for leaf in scratch if leaf.memory_space == pltpu.VMEM]
+    held = sum(math.prod(leaf.shape) * jnp.dtype(leaf.dtype).itemsize for leaf in leaves)
+    args = [
+        pltpu.with_memory_space_constraint(arg, pltpu.HBM) if number in far else arg
+        for number, arg in enumerate(args)
+    ]
     in_specs = [pl.BlockSpec(memory_space=pltpu.SMEM) for _ in scalars]
-    in_specs += [whole(a) for a in args]
+    in_specs += [
+        pl.BlockSpec(memory_space=pltpu.HBM if number in far else pltpu.VMEM)
+        for number in range(len(args))
+    ]
     return pl.pallas_call(
         body,
         out_shape=outs,
-        grid=(1,),
         in_specs=in_specs,
-        out_specs=jax.tree.map(whole, outs),
+        out_specs=jax.tree.map(lambda _: pl.BlockSpec(memory_space=pltpu.VMEM), outs),
         scratch_shapes=scratch,
-        cost_estimate=cost,
-        name=body.__name__ if hasattr(body, "__name__") else None,
+        compiler_params=pltpu.CompilerParams(vmem_limit_bytes=held + (4 << 20)),
+        cost_estimate=pl.CostEstimate(flops=flops, bytes_accessed=held, transcendentals=0),
     )(*scalars, *args)
 
 
-def pack_rows(fields, grp_index, groups):
+def rim_rows(members):
+    return -(-(6 * members + 18) // ROW_TILE) * ROW_TILE
+
+
+def pack_rows(fields, flow, grp_index, groups):
     members, dims, size_x, size_y = fields.shape
     rows = size_x // groups
     planes = members * dims
-    rim = -(-2 * planes // ROW_TILE) * ROW_TILE
+    rim = rim_rows(members)
     shape = jax.ShapeDtypeStruct((planes * rows + rim, size_y), fields.dtype)
 
-    def pack(index, source, *targets):
-        for shift, target in enumerate(targets):
+    def pack(index, source, motion, *refs):
+        targets, singles = refs[:groups], refs[groups : groups + dims]
+        edges, ends, copied, fetched, ended, alone = refs[groups + dims :]
+        last = motion.shape[1] - END_ROWS
+        moves = [
+            pltpu.make_async_copy(
+                motion.at[:, first : first + END_ROWS, :], ends.at[side], ended.at[side]
+            )
+            for side, first in enumerate((0, last))
+        ]
+        for shift in range(groups):
             block = (index[0] + shift) % groups
             start = pl.multiple_of(block * rows, rows)
             above = pl.multiple_of((block + groups - 1) % groups * rows + rows - ROW_TILE, ROW_TILE)
             below = pl.multiple_of((block + 1) % groups * rows, rows)
-            edge = jnp.zeros((rim, size_y), jnp.float32)
-            place = row_index((rim, size_y))
+            for side, place in enumerate((above, below)):
+                moves.append(
+                    pltpu.make_async_copy(
+                        source.at[:, :, pl.ds(place, ROW_TILE), :],
+                        edges.at[shift, side],
+                        fetched.at[shift, side],
+                    )
+                )
+            for plane in range(planes):
+                moves.append(
+                    pltpu.make_async_copy(
+                        source.at[plane // dims, plane % dims, pl.ds(start, rows), :],
+                        targets[shift].at[plane * rows : (plane + 1) * rows, :],
+                        copied.at[shift, plane],
+                    )
+                )
+        lone = [
+            pltpu.make_async_copy(source.at[:, dim], singles[dim], alone.at[dim])
+            for dim in range(dims)
+        ]
+        for move in moves + lone:
+            move.start()
+        place = row_index((rim, size_y))
+        common = jnp.zeros((rim, size_y), jnp.float32)
+        slot = 2 * planes
+        for move in moves[:2]:
+            move.wait()
+        for side, line in enumerate((0, END_ROWS - 1)):
+            for dim in range(dims):
+                rest = ends[side, dim][line : line + 1, :]
+                for _ in range(3):
+                    part = rest.astype(jnp.bfloat16).astype(jnp.float32)
+                    rest = rest - part
+                    common = jnp.where(place == slot, part, common)
+                    slot += 1
+        for move in moves[2:]:
+            move.wait()
+        for shift in range(groups):
+            edge = common
             for member in range(members):
                 for dim in range(dims):
-                    plane = member * dims + dim
-                    target[plane * rows : (plane + 1) * rows, :] = source[
-                        member, dim, pl.ds(start, rows), :
-                    ]
-                    top = source[member, dim, pl.ds(above, ROW_TILE), :].astype(jnp.float32)
-                    bottom = source[member, dim, pl.ds(below, ROW_TILE), :].astype(jnp.float32)
+                    top = edges[shift, 0, member, dim].astype(jnp.float32)
+                    bottom = edges[shift, 1, member, dim].astype(jnp.float32)
                     slot = dim * 2 * members + member * 2
                     edge = jnp.where(place == slot, top[ROW_TILE - 1 :], edge)
                     edge = jnp.where(place == slot + 1, bottom[:1], edge)
-            target[planes * rows :, :] = edge.astype(fields.dtype)
-
-    return run_kernel(pack, [shape] * groups, [fields], [grp_index])
-
-
-def force_rows(blocks, motion, above, below, table, members, field_total):
+            targets[shift][planes * rows :, :] = edge.astype(fields.dtype)
+        for move in lone:
+            move.wait()
+
+    return run_kernel(
+        pack,
+        [shape] * groups
+        + [jax.ShapeDtypeStruct((members, size_x, size_y), fields.dtype)] * dims,
+        [fields, flow],
+        [grp_index],
+        scratch=[
+            pltpu.VMEM((groups, 2, members, dims, ROW_TILE, size_y), fields.dtype),
+            pltpu.VMEM((2, 3, END_ROWS, size_y), flow.dtype),
+            pltpu.SemaphoreType.DMA((groups, planes)),
+            pltpu.SemaphoreType.DMA((groups, 2)),
+            pltpu.SemaphoreType.DMA((2,)),
+            pltpu.SemaphoreType.DMA((dims,)),
+        ],
+        far=(0, 1),
+    )
+
+
+def force_rows(blocks, motion, near, far, sign, table, members, field_total):
     rows, size_y = motion.shape[1:]
     planes = 3 * members
+    rim = rim_rows(members)
 
     def stress_of(sums):
         stretch = stretch_factor((sums[0] + sums[1] + sums[2]) / field_total)
@@ -322,17 +393,18 @@
             for slot, (first, second) in enumerate(TENSOR_PAIRS)
         ]
 
-    def force(*refs):
+    def force(signs, *refs):
         parts = refs[: len(blocks)]
-        flow, top, bottom, table_high, table_low, out, stretch_out, stress, stack = refs[
-            len(blocks) :
-        ]
+        flow, pair, other, tables, out, late, stress, stack = refs[len(blocks) :]
+        side = signs[0].astype(jnp.float32)
         for start in range(0, rows, ROW_TILE):
             sums = [None] * 6
             for part in parts:
                 for member in range(members):
                     vector = [
-                        part[
+                        part[(member * 3 + dim) * rows + start :][:ROW_TILE, :].astype(jnp.float32)
+                        if False
+                        else part[
                             (member * 3 + dim) * rows + start : (member * 3 + dim) * rows
                             + start
                             + ROW_TILE,
@@ -344,12 +416,14 @@
                         term = vector[first] * vector[second]
                         sums[slot] = term if sums[slot] is None else sums[slot] + term
             stretch, values = stress_of(sums)
-            stretch_out[start : start + ROW_TILE, :] = stretch
+            late[3, start : start + ROW_TILE, :] = stretch
             for slot in range(6):
                 stress[slot, start : start + ROW_TILE, :] = values[slot]
         sums = [None] * 6
+        lines = []
         for part in parts:
-            edge = part[planes * rows :, :].astype(jnp.float32)
+            edge = part[planes * rows : planes * rows + rim, :].astype(jnp.float32)
+            lines.append(edge[2 * planes :])
             vector = [edge[dim * 2 * members : (dim + 1) * 2 * members] for dim in range(3)]
             for slot, (first, second) in enumerate(TENSOR_PAIRS):
                 term = vector[first] * vector[second]
@@ -358,6 +432,8 @@
             sum(value[2 * member : 2 * member + 2] for member in range(members)) for value in sums
         ]
         edges = stress_of(sums)[1]
+        bottom = [sum(lines[-1][3 * c + t : 3 * c + t + 1] for t in range(3)) for c in range(3)]
+        top = [sum(lines[1][9 + 3 * c + t : 10 + 3 * c + t] for t in range(3)) for c in range(3)]
         half = 0.5 * TIME_STEP
         place = {0: 0, 1: 1, 2: 4}
         for component in range(3):
@@ -372,22 +448,23 @@
                 row_after(own, bottom[component]) - row_before(own, top[component])
             )
             total = total - flow[1] * lane_difference(own)
-            total = total - (2.0 * flow[2]) * flow[3 + component]
+            rise = side * (pair[component] - other[component])
+            late[component] = 0.5 * rise
+            total = total - flow[2] * rise
             spot = place[component]
             stack[spot * rows : (spot + 1) * rows, :] = own + half * total
             spot = spot + (2 if component < 2 else 1)
             stack[spot * rows : (spot + 1) * rows, :] = half * stress[slot_z]
-        out[...] = dot_split(
-            (table_high[...], table_low[...]), split_value(stack[...]), ((1,), (1,))
-        )
+        out[...] = dot_split((tables[0], tables[1]), split_value(stack[...]), ((1,), (1,)))
 
     return run_kernel(
         force,
         [
             jax.ShapeDtypeStruct((size_y, 6 * rows), jnp.float32),
-            jax.ShapeDtypeStruct((rows, size_y), jnp.float32),
+            jax.ShapeDtypeStruct((4, rows, size_y), jnp.float32),
         ],
-        [*blocks, motion, above, below, *table],
+        [*blocks, motion, near, far, table],
+        [sign],
         scratch=[
             pltpu.VMEM((6, rows, size_y), jnp.float32),
             pltpu.VMEM((6 * rows, size_y), jnp.float32),
@@ -411,7 +488,7 @@
     def join(first, second, lane):
         return jnp.where(lane < rows, first, pltpu.roll(second, rows, 1))
 
-    def solve(index, source, table_high, table_low, out, stack, result):
+    def solve(index, source, tables, out, stack, result):
         lane = lane_index((block, 2 * rows))
         for pair in range(groups // 2):
             both = []
@@ -445,7 +522,7 @@
                 stack[2 * lines + line : 2 * lines + line + block, columns] = join(
                     third, third_b, lane
                 )
-        table_x = (table_high[...], table_low[...])
+        table_x = (tables[2], tables[3])
         result[...] = dot_split(split_value(stack[...]), table_x, ((1,), (0,)))
 
         shape = (block, size_x)
@@ -548,7 +625,7 @@
     return run_kernel(
         solve,
         jax.ShapeDtypeStruct((groups * total_z, block, 4 * rows), jnp.float32),
-        [pencil, *table],
+        [pencil, table],
         [device_index],
         scratch=[
             pltpu.VMEM((3 * lines, size_x), jnp.float32),
@@ -558,41 +635,38 @@
 
 
 def rows_from_waves(spectra, table, rows):
-    size_y = table[0].shape[1]
-
-    def synthesise(source, table_high, table_low, out):
+    size_y = table.shape[2]
+
+    def synthesise(source, tables, out):
         turned = source[...].T[: 3 * rows]
-        value = dot_split(
-            split_value(turned), (table_high[...], table_low[...]), ((1,), (0,))
-        )
+        value = dot_split(split_value(turned), (tables[0], tables[1]), ((1,), (0,)))
         for component in range(3):
             out[component, 0] = value[component * rows : (component + 1) * rows]
 
     return run_kernel(
         synthesise,
         jax.ShapeDtypeStruct((3, 1, rows, size_y), jnp.float32),
-        [spectra, *table],
-    )
-
-
-def advance_fields(fields, paired, passed, motions, stretches, noise, spots, sign):
-    members, dims, size_x, size_y = fields.shape
-    count = len(motions)
+        [spectra, table],
+    )
+
+
+def advance_fields(fields, near, far, motions, lates, noise, grp_index, offsets, sign):
+    members, _, size_x, size_y = fields.shape
+    count = len(offsets)
     rows = size_x // count
     steps = size_x // ROW_TILE
-
-    def advance(spot, signs, kick, *refs):
-        own, near, far = refs[:3]
-        flows = refs[3 : 3 + count]
-        factors = refs[3 + count : 3 + 2 * count]
-        out, plane, factor = refs[3 + 2 * count :]
+    half = 0.5 * TIME_STEP
+
+    def advance(spot, signs, kick, own, *refs):
+        close, remote, refs = refs[:3], refs[3:6], refs[6:]
+        flows, others, (out, plane) = refs[:count], refs[count : 2 * count], refs[2 * count :]
         for number in range(count):
-            start = pl.multiple_of(spot[number] * rows, rows)
-            for slot in range(6):
+            start = pl.multiple_of((spot[0] ^ offsets[number]) * rows, rows)
+            for slot in range(3):
                 plane[slot, pl.ds(start, rows), :] = flows[number][slot]
-            factor[pl.ds(start, rows), :] = factors[number][...]
+            for slot in range(4):
+                plane[3 + slot, pl.ds(start, rows), :] = others[number][slot]
         side = signs[0].astype(jnp.float32)
-        half = 0.5 * TIME_STEP
 
         def step(number, carry):
             start = pl.multiple_of(number * ROW_TILE, ROW_TILE)
@@ -611,7 +685,7 @@
                         TIME_STEP * plane[3 + c, here, :],
                     )
                 )
-            keep = 1.0 - (TIME_STEP / (2.0 * RELAX_TIME)) * factor[here, :]
+            keep = 1.0 - (TIME_STEP / (2.0 * RELAX_TIME)) * plane[6, here, :]
             lift = side * speed[2]
             for member in range(members):
                 vector = [own[member, c, here, :].astype(jnp.float32) for c in range(3)]
@@ -619,9 +693,8 @@
                     first = own[member, c, pl.ds(before, ROW_TILE), :].astype(jnp.float32)
                     last = own[member, c, pl.ds(after, ROW_TILE), :].astype(jnp.float32)
                     value = vector[c]
-                    rise = near[member, c, here, :].astype(jnp.float32) - far[
-                        member, c, here, :
-                    ].astype(jnp.float32)
+                    rise = close[c][member, here, :].astype(jnp.float32)
+                    rise = rise - remote[c][member, here, :].astype(jnp.float32)
                     total = keep * value + NOISE_SCALE * kick[member, c]
                     for j in range(3):
                         total = total + slope[c][j] * vector[j]
@@ -630,21 +703,18 @@
                     )
                     total = total - speed[1] * lane_difference(value)
                     total = total - lift * rise
-                    out[member, c, here, :] = total.astype(jnp.bfloat16)
+                    out[member, c, here, :] = total.astype(out.dtype)
             return carry
 
         lax.fori_loop(0, steps, step, 0)
 
     return run_kernel(
         advance,
-        jax.ShapeDtypeStruct(fields.shape, jnp.bfloat16),
-        [fields, paired, passed, *motions, *stretches],
-        [spots, sign, noise],
-        scratch=[
-            pltpu.VMEM((6, size_x, size_y), jnp.float32),
-            pltpu.VMEM((size_x, size_y), jnp.float32),
-        ],
-        cost=pl.CostEstimate(flops=60000000, bytes_accessed=5000000, transcendentals=0),
+        jax.ShapeDtypeStruct(fields.shape, fields.dtype),
+        [fields, *near, *far, *motions, *lates],
+        [grp_index, sign, noise],
+        scratch=[pltpu.VMEM((7, size_x, size_y), jnp.float32)],
+        flops=200 * members * size_x * size_y,
     )
 
 
@@ -662,7 +732,8 @@
     bit = lax.axis_size(axis) // 2
     found = [(0, value)]
     while bit:
-        found += [(offset ^ bit, flipped(held, axis, bit)) for offset, held in found]
+        for offset, held in list(found):
+            found.append((offset ^ bit, flipped(held, axis, bit)))
         bit //= 2
     return found
 
@@ -672,7 +743,7 @@
     slabs = lax.axis_size("slab")
     grp_index = lax.axis_index("grp")
     slab_index = lax.axis_index("slab")
-    members, dims, _, size_x, size_y = fields.shape
+    members, _, _, size_x, size_y = fields.shape
     rows = velocity.shape[2]
     devices = groups * slabs
     block = size_y // devices
@@ -684,27 +755,31 @@
             for device in range(devices)
         ]
     )
-    table_y = split_table(np.ascontiguousarray(real_basis(size_y).T[order]))
-    table_x = split_table(real_basis(size_x))
+    table = split_tables(np.ascontiguousarray(real_basis(size_y).T[order]), real_basis(size_x))
 
     flow = velocity[:, 0]
-    above = shifted(flow[:, -1:], "grp", 1)
-    below = shifted(flow[:, :1], "grp", -1)
-    lower = shifted(flow, "slab", 1)
-    upper = shifted(flow, "slab", -1)
     plane = fields[:, :, 0]
-    blocks = pack_rows(plane, grp_index.reshape(1), groups)
-    blocks = [blocks[0]] + [shifted(blocks[d], "grp", d) for d in range(1, groups)]
-    paired = flipped(plane, "slab", 1)
-    passed = lax.ppermute(
-        paired, "slab", [(i, (i + (-2 if i % 2 else 2)) % slabs) for i in range(slabs)]
-    )
-    motion = jnp.concatenate([flow, (upper - lower) * 0.5], axis=0)
-    motions = spread(motion, "grp")
-    spectra, stretch = force_rows(
-        blocks, motion, above, below, table_y, members, members * groups
-    )
-    stretches = spread(stretch, "grp")
+    two_up = [(i, (i + (-2 if i % 2 else 2)) % slabs) for i in range(slabs)]
+    sign = (1 - 2 * (slab_index & 1)).reshape(1)
+    packed = pack_rows(plane, flow, grp_index.reshape(1), groups)
+    blocks, parts = packed[:groups], packed[groups:]
+    received = [blocks[0]]
+    for d in range(1, groups):
+        received.append(shifted(blocks[d], "grp", d))
+    flow_near = flipped(flow, "slab", 1)
+    flow_far = lax.ppermute(flow_near, "slab", two_up)
+    two_down = [(target, source) for source, target in two_up]
+    near = []
+    for part in parts:
+        near.append(flipped(part, "slab", 1))
+    hopped = lax.ppermute(parts[0], "slab", two_down)
+    far = [flipped(hopped, "slab", 1)]
+    far.append(lax.ppermute(near[1], "slab", two_up))
+    motions = spread(flow, "grp")
+    spectra, late = force_rows(
+        received, flow, flow_near, flow_far, sign, table, members, members * groups
+    )
+    lates = spread(late, "grp")
     pencil = lax.all_to_all(
         spectra.reshape(devices, block, 6 * rows),
         ("grp", "slab"),
@@ -712,24 +787,25 @@
         concat_axis=0,
         tiled=True,
     )
+    last, pencil = lax.optimization_barrier((near[2], pencil))
+    far.append(lax.ppermute(last, "slab", two_up))
     device_index = (grp_index * slabs + slab_index).reshape(1)
-    solved = solve_pencil(pencil, device_index, table_x, groups, slabs, size_y)
-    spots = jnp.stack([grp_index ^ offset for offset, _ in motions])
-    sign = (1 - 2 * (slab_index % 2)).reshape(1)
+    solved = solve_pencil(pencil, device_index, table, groups, slabs, size_y)
     new_fields = advance_fields(
         plane,
-        paired,
-        passed,
+        near,
+        far,
         [held for _, held in motions],
-        [held for _, held in stretches],
+        [held for _, held in lates],
         noise,
-        spots,
+        grp_index.reshape(1),
+        [offset for offset, _ in motions],
         sign,
     )
     solved = lax.all_to_all(
         solved, ("grp", "slab"), split_axis=0, concat_axis=0, tiled=True
     )
-    new_velocity = rows_from_waves(solved.reshape(size_y, 4 * rows), table_y, rows)
+    new_velocity = rows_from_waves(solved.reshape(size_y, 4 * rows), table, rows)
     return (new_velocity, new_fields[:, :, None])
 
 
@@ -749,18 +825,14 @@
 
 
 def solution(mesh):
+    specs = (P(None, "slab", "grp", None), P("grp", None, "slab", None, None), P("grp", None))
+
+    def mapped(body):
+        return jax.shard_map(body, mesh=mesh, in_specs=specs, out_specs=specs[:2], check_vma=False)
+
     def step(velocity, fields, noise):
-        body = pencil_shards if pencil_fits(mesh, velocity, fields) else shards
-        return jax.shard_map(
-            body,
-            mesh=mesh,
-            in_specs=(
-                P(None, "slab", "grp", None),
-                P("grp", None, "slab", None, None),
-                P("grp", None),
-            ),
-            out_specs=(P(None, "slab", "grp", None), P("grp", None, "slab", None, None)),
-            check_vma=False,
-        )(velocity, fields, noise)
+        if not pencil_fits(mesh, velocity, fields):
+            return mapped(shards)(velocity, fields, noise)
+        return mapped(pencil_shards)(velocity, fields, noise)
 
     return step

time: 88.8 us -> 73.6 us (0.83)
  waiting for transfers between devices: 42.1 us -> 31.6 us
  starting transfers between devices: 25.5 us -> 29.9 us
  Pallas kernels: 15.3 us -> 11.1 us
  local copies, waits for them, and re-layouts: 3.37 us -> 0.02 us
  other arithmetic: 1.45 us -> 0 us
    all_to_all x1, waiting for transfers between devices: 24.9 us -> 4.88 us  [pencil_shards(): lax.all_to_all(spectra.reshape(devices, block, 6 * rows), ('grp', 'slab')...]
    ppermute x1 -> x4, waiting for transfers between devices: 0.01 us -> 14.3 us  [the longest x1 9.24 us: pencil_shards(): far.append(lax.ppermute(near[1], 'slab', two_up))]
    ppermute x7 -> x11, starting transfers between devices: 4.18 us -> 12.2 us  [flipped(): return lax.ppermute(value, axis, [(i, i ^ bit) for i in range(count)])]
    ppermute x7 -> x3, starting transfers between devices: 8.33 us -> 3 us  [shifted(): lax.ppermute(value, axis, [(i, (i + step) % count) for i in range(count)])]
    ppermute x1 -> x4, starting transfers between devices: 1.47 us -> 6.61 us  [the longest x1 3.33 us: pencil_shards(): hopped = lax.ppermute(parts[0], 'slab', two_down)]
    pallas_call x5, Pallas kernels: 15.3 us -> 11.1 us  [run_kernel(): pl.pallas_call(body, out_shape=outs, in_specs=in_specs, out_specs=jax.tre...]
    all_to_all x1, waiting for transfers between devices: 3.65 us -> 0.01 us  [pencil_shards(): lax.all_to_all(solved, ('grp', 'slab'), split_axis=0, concat_axis=0, tile...]
    unnamed x32 -> x8, local copies, waits for them, and re-layouts: 3.37 us -> 0.02 us
  transfers between devices with their start and end apart: 17 -> 20, of which waited for: 7 -> 7; matrix products, arithmetic and copies ran while one was open for 2% -> 0% of each run, Pallas kernels for 11% -> 12%
where the time goes in v1:
time: 73.6 us; the launch traced here: 73.3 us
  waiting for transfers between devices  31.6 us (43%)
  starting transfers between devices  29.9 us (41%)
  Pallas kernels  11.1 us (15%)
    ppermute x11, starting transfers between devices, flipped(): return lax.ppermute(value, axis, [(i, i ^ bit) for i in range(count)])  12.2 us
    pallas_call x5, Pallas kernels, run_kernel(): pl.pallas_call(body, out_shape=outs, in_specs=in_specs, out_specs=jax.tre...  11.1 us
    ppermute x1, waiting for transfers between devices, pencil_shards(): far.append(lax.ppermute(near[1], 'slab', two_up))  9.24 us
    ppermute x3, waiting for transfers between devices, shifted(): lax.ppermute(value, axis, [(i, (i + step) % count) for i in range(count)])  6.59 us
    ppermute x11, waiting for transfers between devices, flipped(): return lax.ppermute(value, axis, [(i, i ^ bit) for i in range(count)])  5.8 us
    all_to_all x1, starting transfers between devices, pencil_shards(): lax.all_to_all(spectra.reshape(devices, block, 6 * rows), ('grp', 'slab')...  5.31 us
    ppermute x1, waiting for transfers between devices, pencil_shards(): far.append(lax.ppermute(last, 'slab', two_up))  5.04 us
    all_to_all x1, waiting for transfers between devices, pencil_shards(): lax.all_to_all(spectra.reshape(devices, block, 6 * rows), ('grp', 'slab')...  4.88 us
  transfers between devices with their start and end apart: 20, of which 7 were waited for; matrix products, arithmetic and copies ran while one was open for 0% of the time, Pallas kernels for 12%

profile of v1, /device:TPU:0, one launch (start us, length us, event | category | flops | bytes accessed | tf_op | source)
XLA Modules:
  0.0 73.3 jit_solution(9981445473241770554)
XLA Ops:
  0.6 0.0 copy-start
  0.6 3.1 %collective-permute-start.4 = (f32[3,64,256]{2,1,0:T(8,128)}, f32[3,64,256]{2,1,0:T(8,128)S(1)}, u32[]{:S(2)}, u32[]{:S(2)}) collective-permute-start(f32[3,64,256]{2,1,0:T(8,128)} %bitcast.12), channel_id=1, source_target_pairs={{0,1},{1,0},{2,3},{3,2},{4,5},{5,4},{6,7},{7,6},{8,9},{9,8},{10,11... | collective-permute-start | bytes 589832 | tf_op jit(solution)/shard_map/ppermute | solution.py:728
  3.7 0.0 copy-start.2
  3.7 2.8 %shard_map.59 = (bf16[416,256]{1,0:T(8,128)(2,1)S(1)}, bf16[416,256]{1,0:T(8,128)(2,1)S(1)}, bf16[416,256]{1,0:T(8,128)(2,1)S(1)}, bf16[416,256]{1,0:T(8,128)(2,...) custom-call(s32[1]{0:T(128)} %bitcast.1.index.spot, ...), custom_call_target="tpu_custom_call" | custom-call | bytes 3063808 | tf_op jit(solution)/shard_map/pallas_call | solution.py:279
  6.5 0.1 collective-permute-start.1
  6.6 1.6 %collective-permute-start.2 = (bf16[416,256]{1,0:T(8,128)(2,1)S(1)}, bf16[416,256]{1,0:T(8,128)(2,1)S(1)}, u32[]{:S(2)}, u32[]{:S(2)}) collective-permute-start(bf16[416,256]{1,0:T(8,128)(2,1)S(1)} %get-tuple-element.16), channel_id=1, source_target_pairs={{0,16},{8,24},{16,0},{24,8},{1,17},{9,25},{17,1},{25,9},{2,18},{10... | collective-permute-start | bytes 638984 | tf_op jit(solution)/shard_map/ppermute | solution.py:723
  8.1 1.4 %collective-permute-start.3 = (bf16[416,256]{1,0:T(8,128)(2,1)S(1)}, bf16[416,256]{1,0:T(8,128)(2,1)S(1)}, u32[]{:S(2)}, u32[]{:S(2)}) collective-permute-start(bf16[416,256]{1,0:T(8,128)(2,1)S(1)} %get-tuple-element.17), channel_id=1, source_target_pairs={{0,24},{8,0},{16,8},{24,16},{1,25},{9,1},{17,9},{25,17},{2,26},{10... | collective-permute-start | bytes 638984 | tf_op jit(solution)/shard_map/ppermute | solution.py:723
  9.5 0.0 collective-permute-done.4.refs_5_
  9.5 1.6 %collective-permute-start.5 = (f32[3,64,256]{2,1,0:T(8,128)S(1)}, f32[3,64,256]{2,1,0:T(8,128)S(1)}, u32[]{:S(2)}, u32[]{:S(2)}) collective-permute-start(f32[3,64,256]{2,1,0:T(8,128)S(1)} %collective-permute-done.4.refs_5_), channel_id=1, source_target_pairs={{0,2},{1,7},{2,4},{3,1},{4,6},{5,3},{6,0},{7,5},{8,10},{9,15},{10,... | collective-permute-start | bytes 589832 | tf_op jit(solution)/shard_map/ppermute | solution.py:770
  11.1 2.4 %collective-permute-done.1.refs_1_ = bf16[416,256]{1,0:T(8,128)(2,1)S(1)} collective-permute-done((bf16[416,256]{1,0:T(8,128)(2,1)S(1)}, bf16[416,256]{1,0:T(8,128)(2,1)S(1)}, u32[]{:S(2)}, u32[]{:S(2)}) %collective-permute-start.1) | collective-permute-done | bytes 213024 | tf_op jit(solution)/shard_map/ppermute | solution.py:723
  13.4 1.3 %collective-permute-done.2.refs_2_ = bf16[416,256]{1,0:T(8,128)(2,1)S(1)} collective-permute-done((bf16[416,256]{1,0:T(8,128)(2,1)S(1)}, bf16[416,256]{1,0:T(8,128)(2,1)S(1)}, u32[]{:S(2)}, u32[]{:S(2)}) %collective-permute-start.2) | collective-permute-done | bytes 213024 | tf_op jit(solution)/shard_map/ppermute | solution.py:723
  14.8 2.9 %collective-permute-done.3.refs_3_ = bf16[416,256]{1,0:T(8,128)(2,1)S(1)} collective-permute-done((bf16[416,256]{1,0:T(8,128)(2,1)S(1)}, bf16[416,256]{1,0:T(8,128)(2,1)S(1)}, u32[]{:S(2)}, u32[]{:S(2)}) %collective-permute-start.3) | collective-permute-done | bytes 213024 | tf_op jit(solution)/shard_map/ppermute | solution.py:723
  17.7 0.0 collective-permute-done.5.refs_6_
  17.7 0.0 copy-done
  17.7 0.0 copy-done.2
  17.7 1.6 %shard_map.60 = (f32[256,384]{1,0:T(8,128)}, f32[4,64,256]{2,1,0:T(8,128)S(1)}) custom-call(s32[1]{0:T(128)} %bitcast.4.signs, bf16[416,256]{1,0:T(8,128)(2,1)S(1)} %get-tuple-element.14.refs_0_, bf16[416,256]{1,0:T(8,128)(2,1)S(1)} %collective-permute-done.1.refs_1_, bf16[416,256]{1,0:T(8,128)(2,1)S(1)} %collective-permute-done.2.refs_2_, ...), custom_call_target="tpu_custom_call" | custom-call | bytes 3407872 | tf_op jit(solution)/shard_map/pallas_call | solution.py:279
  19.3 5.3 %all-to-all-start = ((f32[32,8,384]{2,1,0:T(8,128)}), f32[32,8,384]{2,1,0:T(8,128)S(1)}, u32[]{:S(2)}, u32[]{:S(2)}) async-start(f32[32,8,384]{2,1,0:T(8,128)} %bitcast.5), calls=%async_computation | async-start | bytes 786432 | tf_op jit(solution)/shard_map/all_to_all | solution.py:783
  24.6 1.8 %collective-permute-start = (bf16[2,256,256]{2,1,0:T(8,128)(2,1)S(1)}, bf16[2,256,256]{2,1,0:T(8,128)(2,1)S(1)}, u32[]{:S(2)}, u32[]{:S(2)}) collective-permute-start(bf16[2,256,256]{2,1,0:T(8,128)(2,1)S(1)} %get-tuple-element.13), channel_id=1, source_target_pairs={{0,1},{1,0},{2,3},{3,2},{4,5},{5,4},{6,7},{7,6},{8,9},{9,8},{10,11... | collective-permute-start | bytes 786440 | tf_op jit(solution)/shard_map/ppermute | solution.py:728
  26.4 0.0 collective-permute-start.13
  26.5 1.5 %collective-permute-start.12 = (f32[3,64,256]{2,1,0:T(8,128)S(1)}, f32[3,64,256]{2,1,0:T(8,128)}, u32[]{:S(2)}, u32[]{:S(2)}) collective-permute-start(f32[3,64,256]{2,1,0:T(8,128)S(1)} %bitcast.16), channel_id=1, source_target_pairs={{0,16},{8,24},{16,0},{24,8},{1,17},{9,25},{17,1},{25,9},{2,18},{10... | collective-permute-start | bytes 589832 | tf_op jit(solution)/shard_map/ppermute | solution.py:728
  27.9 0.6 collective-permute-start.7
  28.5 3.3 %collective-permute-start.8 = (bf16[2,256,256]{2,1,0:T(8,128)(2,1)}, bf16[2,256,256]{2,1,0:T(8,128)(2,1)}, u32[]{:S(2)}, u32[]{:S(2)}) collective-permute-start(bf16[2,256,256]{2,1,0:T(8,128)(2,1)} %get-tuple-element.20), channel_id=1, source_target_pairs={{2,0},{7,1},{4,2},{1,3},{6,4},{3,5},{0,6},{5,7},{10,8},{15,9},{12,... | collective-permute-start | bytes 786440 | tf_op jit(solution)/shard_map/ppermute | solution.py:775
  31.8 0.0 collective-permute-done.13.refs_8_
  31.8 0.0 collective-permute-start.6
  31.8 5.8 %collective-permute-done.refs_2_ = bf16[2,256,256]{2,1,0:T(8,128)(2,1)S(1)} collective-permute-done((bf16[2,256,256]{2,1,0:T(8,128)(2,1)S(1)}, bf16[2,256,256]{2,1,0:T(8,128)(2,1)S(1)}, u32[]{:S(2)}, u32[]{:S(2)}) %collective-permute-start) | collective-permute-done | bytes 262176 | tf_op jit(solution)/shard_map/ppermute | solution.py:728
  37.6 1.2 %collective-permute-start.15 = (f32[4,64,256]{2,1,0:T(8,128)S(1)}, f32[4,64,256]{2,1,0:T(8,128)S(1)}, u32[]{:S(2)}, u32[]{:S(2)}) collective-permute-start(f32[4,64,256]{2,1,0:T(8,128)S(1)} %get-tuple-element.23.refs_10_), channel_id=1, source_target_pairs={{0,16},{8,24},{16,0},{24,8},{1,17},{9,25},{17,1},{25,9},{2,18},{10... | collective-permute-start | bytes 786440 | tf_op jit(solution)/shard_map/ppermute | solution.py:728
  38.8 4.9 %all-to-all-done.source = f32[32,8,384]{2,1,0:T(8,128)S(1)} async-done(((f32[32,8,384]{2,1,0:T(8,128)}), f32[32,8,384]{2,1,0:T(8,128)S(1)}, u32[]{:S(2)}, u32[]{:S(2)}) %all-to-all-start) | async-done | bytes 393248 | tf_op jit(solution)/shard_map/all_to_all | solution.py:783
  43.7 0.0 copy-start.1
  43.7 1.6 %shard_map.61 = f32[32,8,256]{2,1,0:T(8,128)} custom-call(s32[1]{0:T(128)} %bitcast.index, f32[32,8,384]{2,1,0:T(8,128)S(1)} %all-to-all-done.source, bf16[4,256,256]{2,1,0:T(8,128)(2,1)S(1)} %copy-done), custom_call_target="tpu_custom_call" | custom-call | bytes 1572864 | tf_op jit(solution)/shard_map/pallas_call | solution.py:279
  45.2 0.0 copy-start.3
  45.2 2.7 %all-to-all-start.1 = ((f32[32,8,256]{2,1,0:T(8,128)}), f32[32,8,256]{2,1,0:T(8,128)S(1)}, u32[]{:S(2)}, u32[]{:S(2)}) async-start(f32[32,8,256]{2,1,0:T(8,128)} %shard_map.61), calls=%async_computation.1 | async-start | bytes 524288 | tf_op jit(solution)/shard_map/all_to_all | solution.py:805
  48.0 0.0 collective-permute-done.12.refs_7_
  48.0 0.2 collective-permute-start.14
  48.1 0.0 collective-permute-done.7.refs_1_
  48.1 1.7 %collective-permute-start.10 = (bf16[2,256,256]{2,1,0:T(8,128)(2,1)S(1)}, bf16[2,256,256]{2,1,0:T(8,128)(2,1)S(1)}, u32[]{:S(2)}, u32[]{:S(2)}) collective-permute-start(bf16[2,256,256]{2,1,0:T(8,128)(2,1)S(1)} %collective-permute-done.7.refs_1_), channel_id=1, source_target_pairs={{0,2},{1,7},{2,4},{3,1},{4,6},{5,3},{6,0},{7,5},{8,10},{9,15},{10,... | collective-permute-start | bytes 786440 | tf_op jit(solution)/shard_map/ppermute | solution.py:777
  49.8 0.0 collective-permute-done.8
  49.8 3.4 %collective-permute-start.9 = (bf16[2,256,256]{2,1,0:T(8,128)(2,1)}, bf16[2,256,256]{2,1,0:T(8,128)(2,1)S(1)}, u32[]{:S(2)}, u32[]{:S(2)}) collective-permute-start(bf16[2,256,256]{2,1,0:T(8,128)(2,1)} %collective-permute-done.8), channel_id=1, source_target_pairs={{0,1},{1,0},{2,3},{3,2},{4,5},{5,4},{6,7},{7,6},{8,9},{9,8},{10,11... | collective-permute-start | bytes 786440 | tf_op jit(solution)/shard_map/ppermute | solution.py:728
  53.3 0.0 collective-permute-done.6.refs_0_
  53.3 0.0 collective-permute-start.16
  53.3 0.0 collective-permute-done.15.refs_11_
  53.3 0.5 collective-permute-start.17
  53.8 0.0 collective-permute-done.14.refs_9_
  53.8 0.0 collective-permute-start.11
  53.8 9.2 %collective-permute-done.10.refs_4_ = bf16[2,256,256]{2,1,0:T(8,128)(2,1)S(1)} collective-permute-done((bf16[2,256,256]{2,1,0:T(8,128)(2,1)S(1)}, bf16[2,256,256]{2,1,0:T(8,128)(2,1)S(1)}, u32[]{:S(2)}, u32[]{:S(2)}) %collective-permute-start.10) | collective-permute-done | bytes 262176 | tf_op jit(solution)/shard_map/ppermute | solution.py:777
  63.0 0.0 collective-permute-done.9.refs_3_
  63.0 0.0 collective-permute-done.16.refs_12_
  63.0 0.0 collective-permute-done.17.refs_13_
  63.1 5.0 %collective-permute-done.11.refs_5_ = bf16[2,256,256]{2,1,0:T(8,128)(2,1)S(1)} collective-permute-done((bf16[2,256,256]{2,1,0:T(8,128)(2,1)S(1)}, bf16[2,256,256]{2,1,0:T(8,128)(2,1)S(1)}, u32[]{:S(2)}, u32[]{:S(2)}) %collective-permute-start.11) | collective-permute-done | bytes 262176 | tf_op jit(solution)/shard_map/ppermute | solution.py:791
  68.1 0.0 copy-done.1
  68.1 0.0 copy-done.3
  68.1 4.2 %shard_map.63 = bf16[2,3,256,256]{3,2,1,0:T(8,128)(2,1)} custom-call(s32[1]{0:T(128)} %bitcast.1.index.spot, s32[1]{0:T(128)} %bitcast.4.signs, f32[2,3]{1,0:T(2,128)S(1)} %copy-done.3, bf16[2,3,256,256]{3,2,1,0:T(8,128)(2,1)S(1)} %bitcast.11, bf16[2,256,256]{2,1,0:T(8,128)(2,1)S(1)} %collective-permute-done.6.refs_0_, ...), custom_call_target="tpu_custom_call" | custom-call | flops 26214400 | bytes 6815744 | tf_op jit(solution)/shard_map/pallas_call | solution.py:279
  72.3 0.0 all-to-all-done.1
  72.3 1.0 %shard_map.62 = f32[3,1,64,256]{3,2,1,0:T(8,128)} custom-call(f32[256,256]{1,0:T(8,128)S(1)} %bitcast.18, bf16[4,256,256]{2,1,0:T(8,128)(2,1)S(1)} %copy-done), custom_call_target="tpu_custom_call" | custom-call | bytes 983040 | tf_op jit(solution)/shard_map/pallas_call | solution.py:279
Async XLA Ops:
  0.6 17.1 %copy-start = (bf16[4,256,256]{2,1,0:T(8,128)(2,1)S(1)}, bf16[4,256,256]{2,1,0:T(8,128)(2,1)}, u32[]{:S(2)}) copy-start(bf16[4,256,256]{2,1,0:T(8,128)(2,1)} %constant.16.clone.refs_7_.tables) | copy-start | bytes 1572868
  0.6 8.9 %collective-permute-start.4 = (f32[3,64,256]{2,1,0:T(8,128)}, f32[3,64,256]{2,1,0:T(8,128)S(1)}, u32[]{:S(2)}, u32[]{:S(2)}) collective-permute-start(f32[3,64,256]{2,1,0:T(8,128)} %bitcast.12), channel_id=1, source_target_pairs={{0,1},{1,0},{2,3},{3,2},{4,5},{5,4},{6,7},{7,6},{8,9},{9,8},{10,11... | collective-permute-start | bytes 589832 | tf_op jit(solution)/shard_map/ppermute | solution.py:728
  3.7 14.0 %copy-start.2 = (f32[3,1,64,256]{3,2,1,0:T(8,128)S(1)}, f32[3,1,64,256]{3,2,1,0:T(8,128)}, u32[]{:S(2)}) copy-start(f32[3,1,64,256]{3,2,1,0:T(8,128)} %param.4) | copy-start | bytes 589828
  6.5 6.9 %collective-permute-start.1 = (bf16[416,256]{1,0:T(8,128)(2,1)S(1)}, bf16[416,256]{1,0:T(8,128)(2,1)S(1)}, u32[]{:S(2)}, u32[]{:S(2)}) collective-permute-start(bf16[416,256]{1,0:T(8,128)(2,1)S(1)} %get-tuple-element.15), channel_id=1, source_target_pairs={{0,8},{8,16},{16,24},{24,0},{1,9},{9,17},{17,25},{25,1},{2,10},{10... | collective-permute-start | bytes 638984 | tf_op jit(solution)/shard_map/ppermute | solution.py:723
  6.6 8.2 %collective-permute-start.2 = (bf16[416,256]{1,0:T(8,128)(2,1)S(1)}, bf16[416,256]{1,0:T(8,128)(2,1)S(1)}, u32[]{:S(2)}, u32[]{:S(2)}) collective-permute-start(bf16[416,256]{1,0:T(8,128)(2,1)S(1)} %get-tuple-element.16), channel_id=1, source_target_pairs={{0,16},{8,24},{16,0},{24,8},{1,17},{9,25},{17,1},{25,9},{2,18},{10... | collective-permute-start | bytes 638984 | tf_op jit(solution)/shard_map/ppermute | solution.py:723
  8.1 9.6 %collective-permute-start.3 = (bf16[416,256]{1,0:T(8,128)(2,1)S(1)}, bf16[416,256]{1,0:T(8,128)(2,1)S(1)}, u32[]{:S(2)}, u32[]{:S(2)}) collective-permute-start(bf16[416,256]{1,0:T(8,128)(2,1)S(1)} %get-tuple-element.17), channel_id=1, source_target_pairs={{0,24},{8,0},{16,8},{24,16},{1,25},{9,1},{17,9},{25,17},{2,26},{10... | collective-permute-start | bytes 638984 | tf_op jit(solution)/shard_map/ppermute | solution.py:723
  9.5 8.2 %collective-permute-start.5 = (f32[3,64,256]{2,1,0:T(8,128)S(1)}, f32[3,64,256]{2,1,0:T(8,128)S(1)}, u32[]{:S(2)}, u32[]{:S(2)}) collective-permute-start(f32[3,64,256]{2,1,0:T(8,128)S(1)} %collective-permute-done.4.refs_5_), channel_id=1, source_target_pairs={{0,2},{1,7},{2,4},{3,1},{4,6},{5,3},{6,0},{7,5},{8,10},{9,15},{10,... | collective-permute-start | bytes 589832 | tf_op jit(solution)/shard_map/ppermute | solution.py:770
  19.3 24.4 %all-to-all-start = ((f32[32,8,384]{2,1,0:T(8,128)}), f32[32,8,384]{2,1,0:T(8,128)S(1)}, u32[]{:S(2)}, u32[]{:S(2)}) async-start(f32[32,8,384]{2,1,0:T(8,128)} %bitcast.5), calls=%async_computation | async-start | bytes 786432 | tf_op jit(solution)/shard_map/all_to_all | solution.py:783
  24.6 13.0 %collective-permute-start = (bf16[2,256,256]{2,1,0:T(8,128)(2,1)S(1)}, bf16[2,256,256]{2,1,0:T(8,128)(2,1)S(1)}, u32[]{:S(2)}, u32[]{:S(2)}) collective-permute-start(bf16[2,256,256]{2,1,0:T(8,128)(2,1)S(1)} %get-tuple-element.13), channel_id=1, source_target_pairs={{0,1},{1,0},{2,3},{3,2},{4,5},{5,4},{6,7},{7,6},{8,9},{9,8},{10,11... | collective-permute-start | bytes 786440 | tf_op jit(solution)/shard_map/ppermute | solution.py:728
  26.4 5.4 %collective-permute-start.13 = (f32[3,64,256]{2,1,0:T(8,128)S(1)}, f32[3,64,256]{2,1,0:T(8,128)S(1)}, u32[]{:S(2)}, u32[]{:S(2)}) collective-permute-start(f32[3,64,256]{2,1,0:T(8,128)S(1)} %bitcast.15), channel_id=1, source_target_pairs={{0,8},{8,0},{16,24},{24,16},{1,9},{9,1},{17,25},{25,17},{2,10},{10... | collective-permute-start | bytes 589832 | tf_op jit(solution)/shard_map/ppermute | solution.py:728
  26.5 21.5 %collective-permute-start.12 = (f32[3,64,256]{2,1,0:T(8,128)S(1)}, f32[3,64,256]{2,1,0:T(8,128)}, u32[]{:S(2)}, u32[]{:S(2)}) collective-permute-start(f32[3,64,256]{2,1,0:T(8,128)S(1)} %bitcast.16), channel_id=1, source_target_pairs={{0,16},{8,24},{16,0},{24,8},{1,17},{9,25},{17,1},{25,9},{2,18},{10... | collective-permute-start | bytes 589832 | tf_op jit(solution)/shard_map/ppermute | solution.py:728
  27.9 20.2 %collective-permute-start.7 = (bf16[2,256,256]{2,1,0:T(8,128)(2,1)}, bf16[2,256,256]{2,1,0:T(8,128)(2,1)S(1)}, u32[]{:S(2)}, u32[]{:S(2)}) collective-permute-start(bf16[2,256,256]{2,1,0:T(8,128)(2,1)} %get-tuple-element.21), channel_id=1, source_target_pairs={{0,1},{1,0},{2,3},{3,2},{4,5},{5,4},{6,7},{7,6},{8,9},{9,8},{10,11... | collective-permute-start | bytes 786440 | tf_op jit(solution)/shard_map/ppermute | solution.py:728
  28.5 21.4 %collective-permute-start.8 = (bf16[2,256,256]{2,1,0:T(8,128)(2,1)}, bf16[2,256,256]{2,1,0:T(8,128)(2,1)}, u32[]{:S(2)}, u32[]{:S(2)}) collective-permute-start(bf16[2,256,256]{2,1,0:T(8,128)(2,1)} %get-tuple-element.20), channel_id=1, source_target_pairs={{2,0},{7,1},{4,2},{1,3},{6,4},{3,5},{0,6},{5,7},{10,8},{15,9},{12,... | collective-permute-start | bytes 786440 | tf_op jit(solution)/shard_map/ppermute | solution.py:775
  31.8 21.5 %collective-permute-start.6 = (bf16[2,256,256]{2,1,0:T(8,128)(2,1)}, bf16[2,256,256]{2,1,0:T(8,128)(2,1)S(1)}, u32[]{:S(2)}, u32[]{:S(2)}) collective-permute-start(bf16[2,256,256]{2,1,0:T(8,128)(2,1)} %get-tuple-element.20), channel_id=1, source_target_pairs={{0,1},{1,0},{2,3},{3,2},{4,5},{5,4},{6,7},{7,6},{8,9},{9,8},{10,11... | collective-permute-start | bytes 786440 | tf_op jit(solution)/shard_map/ppermute | solution.py:728
  37.6 15.7 %collective-permute-start.15 = (f32[4,64,256]{2,1,0:T(8,128)S(1)}, f32[4,64,256]{2,1,0:T(8,128)S(1)}, u32[]{:S(2)}, u32[]{:S(2)}) collective-permute-start(f32[4,64,256]{2,1,0:T(8,128)S(1)} %get-tuple-element.23.refs_10_), channel_id=1, source_target_pairs={{0,16},{8,24},{16,0},{24,8},{1,17},{9,25},{17,1},{25,9},{2,18},{10... | collective-permute-start | bytes 786440 | tf_op jit(solution)/shard_map/ppermute | solution.py:728
  43.7 24.4 %copy-start.1 = (bf16[2,3,1,256,256]{4,3,2,1,0:T(8,128)(2,1)S(1)}, bf16[2,3,1,256,256]{4,3,2,1,0:T(8,128)(2,1)}, u32[]{:S(2)}) copy-start(bf16[2,3,1,256,256]{4,3,2,1,0:T(8,128)(2,1)} %param.5) | copy-start | bytes 2359300
  45.2 22.9 %copy-start.3 = (f32[2,3]{1,0:T(2,128)S(1)}, f32[2,3]{1,0:T(2,128)}, u32[]{:S(2)}) copy-start(f32[2,3]{1,0:T(2,128)} %kick.1) | copy-start | bytes 76
  45.2 27.1 %all-to-all-start.1 = ((f32[32,8,256]{2,1,0:T(8,128)}), f32[32,8,256]{2,1,0:T(8,128)S(1)}, u32[]{:S(2)}, u32[]{:S(2)}) async-start(f32[32,8,256]{2,1,0:T(8,128)} %shard_map.61), calls=%async_computation.1 | async-start | bytes 524288 | tf_op jit(solution)/shard_map/all_to_all | solution.py:805
  48.0 5.8 %collective-permute-start.14 = (f32[3,64,256]{2,1,0:T(8,128)}, f32[3,64,256]{2,1,0:T(8,128)S(1)}, u32[]{:S(2)}, u32[]{:S(2)}) collective-permute-start(f32[3,64,256]{2,1,0:T(8,128)} %collective-permute-done.12.refs_7_), channel_id=1, source_target_pairs={{0,8},{8,0},{16,24},{24,16},{1,9},{9,1},{17,25},{25,17},{2,10},{10... | collective-permute-start | bytes 589832 | tf_op jit(solution)/shard_map/ppermute | solution.py:728
  48.1 14.9 %collective-permute-start.10 = (bf16[2,256,256]{2,1,0:T(8,128)(2,1)S(1)}, bf16[2,256,256]{2,1,0:T(8,128)(2,1)S(1)}, u32[]{:S(2)}, u32[]{:S(2)}) collective-permute-start(bf16[2,256,256]{2,1,0:T(8,128)(2,1)S(1)} %collective-permute-done.7.refs_1_), channel_id=1, source_target_pairs={{0,2},{1,7},{2,4},{3,1},{4,6},{5,3},{6,0},{7,5},{8,10},{9,15},{10,... | collective-permute-start | bytes 786440 | tf_op jit(solution)/shard_map/ppermute | solution.py:777
  49.8 13.2 %collective-permute-start.9 = (bf16[2,256,256]{2,1,0:T(8,128)(2,1)}, bf16[2,256,256]{2,1,0:T(8,128)(2,1)S(1)}, u32[]{:S(2)}, u32[]{:S(2)}) collective-permute-start(bf16[2,256,256]{2,1,0:T(8,128)(2,1)} %collective-permute-done.8), channel_id=1, source_target_pairs={{0,1},{1,0},{2,3},{3,2},{4,5},{5,4},{6,7},{7,6},{8,9},{9,8},{10,11... | collective-permute-start | bytes 786440 | tf_op jit(solution)/shard_map/ppermute | solution.py:728
  53.3 9.8 %collective-permute-start.16 = (f32[4,64,256]{2,1,0:T(8,128)S(1)}, f32[4,64,256]{2,1,0:T(8,128)S(1)}, u32[]{:S(2)}, u32[]{:S(2)}) collective-permute-start(f32[4,64,256]{2,1,0:T(8,128)S(1)} %get-tuple-element.23.refs_10_), channel_id=1, source_target_pairs={{0,8},{8,0},{16,24},{24,16},{1,9},{9,1},{17,25},{25,17},{2,10},{10... | collective-permute-start | bytes 786440 | tf_op jit(solution)/shard_map/ppermute | solution.py:728
  53.3 9.8 %collective-permute-start.17 = (f32[4,64,256]{2,1,0:T(8,128)S(1)}, f32[4,64,256]{2,1,0:T(8,128)S(1)}, u32[]{:S(2)}, u32[]{:S(2)}) collective-permute-start(f32[4,64,256]{2,1,0:T(8,128)S(1)} %collective-permute-done.15.refs_11_), channel_id=1, source_target_pairs={{0,8},{8,0},{16,24},{24,16},{1,9},{9,1},{17,25},{25,17},{2,10},{10... | collective-permute-start | bytes 786440 | tf_op jit(solution)/shard_map/ppermute | solution.py:728
  53.8 14.3 %collective-permute-start.11 = (bf16[2,256,256]{2,1,0:T(8,128)(2,1)S(1)}, bf16[2,256,256]{2,1,0:T(8,128)(2,1)S(1)}, u32[]{:S(2)}, u32[]{:S(2)}) collective-permute-start(bf16[2,256,256]{2,1,0:T(8,128)(2,1)S(1)} %collective-permute-done.refs_2_), channel_id=1, source_target_pairs={{0,2},{1,7},{2,4},{3,1},{4,6},{5,3},{6,0},{7,5},{8,10},{9,15},{10,... | collective-permute-start | bytes 786440 | tf_op jit(solution)/shard_map/ppermute | solution.py:791

commit v2 on v1

--- a/solution.py
+++ b/solution.py
@@ -263,7 +263,7 @@
     return pltpu.roll(block, lanes - 1, 1) - pltpu.roll(block, 1, 1)
 
 
-def run_kernel(body, outs, args, scalars=(), scratch=(), flops=0, far=()):
+def run_kernel(body, outs, args, scalars=(), scratch=(), flops=0, far=(), far_outs=(), aliases=None):
     leaves = list(args) + jax.tree.leaves(outs)
     leaves += [leaf for leaf in scratch if leaf.memory_space == pltpu.VMEM]
     held = sum(math.prod(leaf.shape) * jnp.dtype(leaf.dtype).itemsize for leaf in leaves)
@@ -271,6 +271,9 @@
         pltpu.with_memory_space_constraint(arg, pltpu.HBM) if number in far else arg
         for number, arg in enumerate(args)
     ]
+    spaces = jax.tree.map(lambda _: pl.BlockSpec(memory_space=pltpu.VMEM), outs)
+    for number in far_outs:
+        spaces[number] = pl.BlockSpec(memory_space=pltpu.HBM)
     in_specs = [pl.BlockSpec(memory_space=pltpu.SMEM) for _ in scalars]
     in_specs += [
         pl.BlockSpec(memory_space=pltpu.HBM if number in far else pltpu.VMEM)
@@ -280,8 +283,9 @@
         body,
         out_shape=outs,
         in_specs=in_specs,
-        out_specs=jax.tree.map(lambda _: pl.BlockSpec(memory_space=pltpu.VMEM), outs),
+        out_specs=spaces,
         scratch_shapes=scratch,
+        input_output_aliases=aliases or {},
         compiler_params=pltpu.CompilerParams(vmem_limit_bytes=held + (4 << 20)),
         cost_estimate=pl.CostEstimate(flops=flops, bytes_accessed=held, transcendentals=0),
     )(*scalars, *args)
@@ -611,20 +615,23 @@
             columns = slice(group // 2 * 2 * rows, (group // 2 + 1) * 2 * rows)
             for z in range(total_z):
                 line = z * block
-                first, second, third = [
+                held = [
                     result[c * lines + line : c * lines + line + block, columns] for c in range(3)
                 ]
-                if group % 2 == 0:
-                    front = join(first, second, lane)
-                else:
-                    front = jnp.where(lane < rows, pltpu.roll(first, rows, 1), second)
-                    third = pltpu.roll(third, rows, 1)
-                out[group * total_z + z, :, : 2 * rows] = front
-                out[group * total_z + z, :, 2 * rows :] = third
+                turned = [pltpu.roll(value, rows, 1) for value in held]
+                low, high = (held, turned) if group % 2 == 0 else (turned, held)
+                tiles = (
+                    jnp.where(lane < rows, low[0], high[1]),
+                    jnp.where(lane < rows, low[2], pltpu.roll(high[0], pairs, 0)),
+                    pltpu.roll(jnp.where(lane < rows, low[1], high[2]), pairs, 0),
+                )
+                for number, tile in enumerate(tiles):
+                    spot = slice(number * 2 * rows, (number + 1) * 2 * rows)
+                    out[group * total_z + z, :, spot] = tile[:pairs]
 
     return run_kernel(
         solve,
-        jax.ShapeDtypeStruct((groups * total_z, block, 4 * rows), jnp.float32),
+        jax.ShapeDtypeStruct((groups * total_z, pairs, 6 * rows), jnp.float32),
         [pencil, table],
         [device_index],
         scratch=[
@@ -635,11 +642,17 @@
 
 
 def rows_from_waves(spectra, table, rows):
+    devices, pairs, lanes = spectra.shape
     size_y = table.shape[2]
-
-    def synthesise(source, tables, out):
-        turned = source[...].T[: 3 * rows]
-        value = dot_split(split_value(turned), (tables[0], tables[1]), ((1,), (0,)))
+    joined = max(8 // pairs, 1)
+
+    def synthesise(source, tables, out, stack):
+        for first in range(0, devices, joined):
+            blocks = [source[device] for device in range(first, first + joined)]
+            stack[first * pairs : (first + joined) * pairs, :] = jnp.concatenate(blocks, axis=0)
+        turned = stack[...].T
+        waves = jnp.concatenate([turned[: 3 * rows], turned[3 * rows :]], axis=1)
+        value = dot_split(split_value(waves), (tables[2], tables[3]), ((1,), (1,)))
         for component in range(3):
             out[component, 0] = value[component * rows : (component + 1) * rows]
 
@@ -647,6 +660,7 @@
         synthesise,
         jax.ShapeDtypeStruct((3, 1, rows, size_y), jnp.float32),
         [spectra, table],
+        scratch=[pltpu.VMEM((devices * pairs, lanes), jnp.float32)],
     )
 
 
@@ -658,8 +672,9 @@
     half = 0.5 * TIME_STEP
 
     def advance(spot, signs, kick, own, *refs):
-        close, remote, refs = refs[:3], refs[3:6], refs[6:]
-        flows, others, (out, plane) = refs[:count], refs[count : 2 * count], refs[2 * count :]
+        close, remote, refs = refs[:2], refs[2:4], refs[4:]
+        flows, others, refs = refs[:count], refs[count : 2 * count], refs[2 * count :]
+        out, rest, pace, plane, ready, sent = refs
         for number in range(count):
             start = pl.multiple_of((spot[0] ^ offsets[number]) * rows, rows)
             for slot in range(3):
@@ -687,14 +702,13 @@
                 )
             keep = 1.0 - (TIME_STEP / (2.0 * RELAX_TIME)) * plane[6, here, :]
             lift = side * speed[2]
+            pace[here, :] = lift
             for member in range(members):
                 vector = [own[member, c, here, :].astype(jnp.float32) for c in range(3)]
                 for c in range(3):
                     first = own[member, c, pl.ds(before, ROW_TILE), :].astype(jnp.float32)
                     last = own[member, c, pl.ds(after, ROW_TILE), :].astype(jnp.float32)
                     value = vector[c]
-                    rise = close[c][member, here, :].astype(jnp.float32)
-                    rise = rise - remote[c][member, here, :].astype(jnp.float32)
                     total = keep * value + NOISE_SCALE * kick[member, c]
                     for j in range(3):
                         total = total + slope[c][j] * vector[j]
@@ -702,20 +716,66 @@
                         row_after(value, last[:1]) - row_before(value, first[ROW_TILE - 1 :])
                     )
                     total = total - speed[1] * lane_difference(value)
-                    total = total - lift * rise
-                    out[member, c, here, :] = total.astype(out.dtype)
+                    if c == 2:
+                        rest[member, here, :] = total
+                        continue
+                    rise = close[c][member, here, :].astype(jnp.float32)
+                    rise = rise - remote[c][member, here, :].astype(jnp.float32)
+                    ready[c, member, here, :] = (total - lift * rise).astype(ready.dtype)
             return carry
 
         lax.fori_loop(0, steps, step, 0)
+        moves = [
+            pltpu.make_async_copy(ready.at[c], out.at[:, c], sent.at[c]) for c in range(2)
+        ]
+        for move in moves:
+            move.start()
+        for move in moves:
+            move.wait()
 
     return run_kernel(
         advance,
-        jax.ShapeDtypeStruct(fields.shape, fields.dtype),
+        [
+            jax.ShapeDtypeStruct(fields.shape, fields.dtype),
+            jax.ShapeDtypeStruct((members, size_x, size_y), jnp.float32),
+            jax.ShapeDtypeStruct((size_x, size_y), jnp.float32),
+        ],
         [fields, *near, *far, *motions, *lates],
         [grp_index, sign, noise],
-        scratch=[pltpu.VMEM((7, size_x, size_y), jnp.float32)],
+        scratch=[
+            pltpu.VMEM((7, size_x, size_y), jnp.float32),
+            pltpu.VMEM((2, members, size_x, size_y), fields.dtype),
+            pltpu.SemaphoreType.DMA((2,)),
+        ],
+        far_outs=(0,),
         flops=200 * members * size_x * size_y,
     )
+
+
+def finish_fields(fields, rest, pace, near, far):
+    members, size_x, size_y = rest.shape
+
+    def finish(partial, speed, close, remote, _, out, ready, sent):
+        for member in range(members):
+            rise = close[member].astype(jnp.float32) - remote[member].astype(jnp.float32)
+            ready[member] = (partial[member] - speed[...] * rise).astype(ready.dtype)
+        move = pltpu.make_async_copy(ready, out.at[:, 2], sent)
+        move.start()
+        move.wait()
+
+    return run_kernel(
+        finish,
+        [jax.ShapeDtypeStruct(fields.shape, fields.dtype)],
+        [rest, pace, near, far, fields],
+        scratch=[
+            pltpu.VMEM((members, size_x, size_y), fields.dtype),
+            pltpu.SemaphoreType.DMA(()),
+        ],
+        flops=4 * members * size_x * size_y,
+        far=(4,),
+        far_outs=(0,),
+        aliases={4: 0},
+    )[0]
 
 
 def shifted(value, axis, step):
@@ -791,10 +851,10 @@
     far.append(lax.ppermute(last, "slab", two_up))
     device_index = (grp_index * slabs + slab_index).reshape(1)
     solved = solve_pencil(pencil, device_index, table, groups, slabs, size_y)
-    new_fields = advance_fields(
+    new_fields, rest, pace = advance_fields(
         plane,
-        near,
-        far,
+        near[:2],
+        far[:2],
         [held for _, held in motions],
         [held for _, held in lates],
         noise,
@@ -802,10 +862,11 @@
         [offset for offset, _ in motions],
         sign,
     )
+    new_fields = finish_fields(new_fields, rest, pace, near[2], far[2])
     solved = lax.all_to_all(
         solved, ("grp", "slab"), split_axis=0, concat_axis=0, tiled=True
     )
-    new_velocity = rows_from_waves(solved.reshape(size_y, 4 * rows), table, rows)
+    new_velocity = rows_from_waves(solved, table, rows)
     return (new_velocity, new_fields[:, :, None])
 
 
@@ -814,6 +875,7 @@
     size_z, size_x, size_y = velocity.shape[1:]
     return (
         size_z == slabs
+        and size_x == size_y
         and slabs % 2 == 0
         and groups >= 2
         and groups & (groups - 1) == 0

time: 73.6 us -> 69.3 us (0.942)
  waiting for transfers between devices: 31.6 us -> 25.6 us
  Pallas kernels: 11.1 us -> 12.1 us
    ppermute x1, waiting for transfers between devices: 9.24 us -> 3.45 us  [pencil_shards(): far.append(lax.ppermute(near[1], 'slab', two_up))]
    ppermute x1, waiting for transfers between devices: 5.04 us -> 0.82 us  [pencil_shards(): far.append(lax.ppermute(last, 'slab', two_up))]
    ppermute x11, waiting for transfers between devices: 5.8 us -> 9.3 us  [flipped(): return lax.ppermute(value, axis, [(i, i ^ bit) for i in range(count)])]
    ppermute x1, starting transfers between devices: 0.01 us -> 1.53 us  [pencil_shards(): far.append(lax.ppermute(last, 'slab', two_up))]
    ppermute x11, starting transfers between devices: 12.2 us -> 10.8 us  [flipped(): return lax.ppermute(value, axis, [(i, i ^ bit) for i in range(count)])]
    pallas_call x5 -> x6, Pallas kernels: 11.1 us -> 12.1 us  [run_kernel(): pl.pallas_call(body, out_shape=outs, in_specs=in_specs, out_specs=spaces,...]
  transfers between devices with their start and end apart: 20 -> 20, of which waited for: 7 -> 9; matrix products, arithmetic and copies ran while one was open for 0% -> 0% of each run, Pallas kernels for 12% -> 14%
where the time goes in v2:
time: 69.3 us; the launch traced here: 69 us
  starting transfers between devices  29.8 us (43%)
  waiting for transfers between devices  25.6 us (37%)
  Pallas kernels  12.1 us (17%)
  between operations  0.75 us (1%)
  local copies, waits for them, and re-layouts  0.7 us (1%)
    pallas_call x6, Pallas kernels, run_kernel(): pl.pallas_call(body, out_shape=outs, in_specs=in_specs, out_specs=spaces,...  12.1 us
    ppermute x11, starting transfers between devices, flipped(): return lax.ppermute(value, axis, [(i, i ^ bit) for i in range(count)])  10.8 us
    ppermute x11, waiting for transfers between devices, flipped(): return lax.ppermute(value, axis, [(i, i ^ bit) for i in range(count)])  9.3 us
    ppermute x3, waiting for transfers between devices, shifted(): lax.ppermute(value, axis, [(i, (i + step) % count) for i in range(count)])  6.59 us
    all_to_all x1, waiting for transfers between devices, pencil_shards(): lax.all_to_all(spectra.reshape(devices, block, 6 * rows), ('grp', 'slab')...  5.46 us
    all_to_all x1, starting transfers between devices, pencil_shards(): lax.all_to_all(spectra.reshape(devices, block, 6 * rows), ('grp', 'slab')...  5.32 us
    ppermute x1, waiting for transfers between devices, pencil_shards(): far.append(lax.ppermute(near[1], 'slab', two_up))  3.45 us
    ppermute x1, starting transfers between devices, pencil_shards(): hopped = lax.ppermute(parts[0], 'slab', two_down)  3.36 us
  transfers between devices with their start and end apart: 20, of which 9 were waited for; matrix products, arithmetic and copies ran while one was open for 0% of the time, Pallas kernels for 14%

profile of v2, /device:TPU:0, one launch (start us, length us, event | category | flops | bytes accessed | tf_op | source)
XLA Modules:
  0.0 69.0 jit_solution(16389698688858999146)
XLA Ops:
  0.6 0.0 copy-start
  0.6 3.1 %collective-permute-start.4 = (f32[3,64,256]{2,1,0:T(8,128)}, f32[3,64,256]{2,1,0:T(8,128)S(1)}, u32[]{:S(2)}, u32[]{:S(2)}) collective-permute-start(f32[3,64,256]{2,1,0:T(8,128)} %bitcast.11), channel_id=1, source_target_pairs={{0,1},{1,0},{2,3},{3,2},{4,5},{5,4},{6,7},{7,6},{8,9},{9,8},{10,11... | collective-permute-start | bytes 589832 | tf_op jit(solution)/shard_map/ppermute | solution.py:788
  3.7 0.0 copy-start.2
  3.7 2.9 %shard_map.59 = (bf16[416,256]{1,0:T(8,128)(2,1)S(1)}, bf16[416,256]{1,0:T(8,128)(2,1)S(1)}, bf16[416,256]{1,0:T(8,128)(2,1)S(1)}, bf16[416,256]{1,0:T(8,128)(2,...) custom-call(s32[1]{0:T(128)} %bitcast.1.index.spot, ...), custom_call_target="tpu_custom_call" | custom-call | bytes 3063808 | tf_op jit(solution)/shard_map/pallas_call | solution.py:282
  6.6 0.1 collective-permute-start.1
  6.7 1.6 %collective-permute-start.2 = (bf16[416,256]{1,0:T(8,128)(2,1)S(1)}, bf16[416,256]{1,0:T(8,128)(2,1)S(1)}, u32[]{:S(2)}, u32[]{:S(2)}) collective-permute-start(bf16[416,256]{1,0:T(8,128)(2,1)S(1)} %get-tuple-element.19), channel_id=1, source_target_pairs={{0,16},{8,24},{16,0},{24,8},{1,17},{9,25},{17,1},{25,9},{2,18},{10... | collective-permute-start | bytes 638984 | tf_op jit(solution)/shard_map/ppermute | solution.py:783
  8.2 1.4 %collective-permute-start.3 = (bf16[416,256]{1,0:T(8,128)(2,1)S(1)}, bf16[416,256]{1,0:T(8,128)(2,1)S(1)}, u32[]{:S(2)}, u32[]{:S(2)}) collective-permute-start(bf16[416,256]{1,0:T(8,128)(2,1)S(1)} %get-tuple-element.20), channel_id=1, source_target_pairs={{0,24},{8,0},{16,8},{24,16},{1,25},{9,1},{17,9},{25,17},{2,26},{10... | collective-permute-start | bytes 638984 | tf_op jit(solution)/shard_map/ppermute | solution.py:783
  9.6 0.0 collective-permute-done.4.refs_5_
  9.6 1.6 %collective-permute-start.5 = (f32[3,64,256]{2,1,0:T(8,128)S(1)}, f32[3,64,256]{2,1,0:T(8,128)S(1)}, u32[]{:S(2)}, u32[]{:S(2)}) collective-permute-start(f32[3,64,256]{2,1,0:T(8,128)S(1)} %collective-permute-done.4.refs_5_), channel_id=1, source_target_pairs={{0,2},{1,7},{2,4},{3,1},{4,6},{5,3},{6,0},{7,5},{8,10},{9,15},{10,... | collective-permute-start | bytes 589832 | tf_op jit(solution)/shard_map/ppermute | solution.py:830
  11.2 2.4 %collective-permute-done.1.refs_1_ = bf16[416,256]{1,0:T(8,128)(2,1)S(1)} collective-permute-done((bf16[416,256]{1,0:T(8,128)(2,1)S(1)}, bf16[416,256]{1,0:T(8,128)(2,1)S(1)}, u32[]{:S(2)}, u32[]{:S(2)}) %collective-permute-start.1) | collective-permute-done | bytes 213024 | tf_op jit(solution)/shard_map/ppermute | solution.py:783
  13.6 1.3 %collective-permute-done.2.refs_2_ = bf16[416,256]{1,0:T(8,128)(2,1)S(1)} collective-permute-done((bf16[416,256]{1,0:T(8,128)(2,1)S(1)}, bf16[416,256]{1,0:T(8,128)(2,1)S(1)}, u32[]{:S(2)}, u32[]{:S(2)}) %collective-permute-start.2) | collective-permute-done | bytes 213024 | tf_op jit(solution)/shard_map/ppermute | solution.py:783
  14.9 2.9 %collective-permute-done.3.refs_3_ = bf16[416,256]{1,0:T(8,128)(2,1)S(1)} collective-permute-done((bf16[416,256]{1,0:T(8,128)(2,1)S(1)}, bf16[416,256]{1,0:T(8,128)(2,1)S(1)}, u32[]{:S(2)}, u32[]{:S(2)}) %collective-permute-start.3) | collective-permute-done | bytes 213024 | tf_op jit(solution)/shard_map/ppermute | solution.py:783
  17.8 0.0 collective-permute-done.5.refs_6_
  17.8 0.0 copy-done
  17.8 0.0 copy-done.2
  17.8 1.6 %shard_map.60 = (f32[256,384]{1,0:T(8,128)}, f32[4,64,256]{2,1,0:T(8,128)S(1)}) custom-call(s32[1]{0:T(128)} %bitcast.4.signs, bf16[416,256]{1,0:T(8,128)(2,1)S(1)} %get-tuple-element.17.refs_0_, bf16[416,256]{1,0:T(8,128)(2,1)S(1)} %collective-permute-done.1.refs_1_, bf16[416,256]{1,0:T(8,128)(2,1)S(1)} %collective-permute-done.2.refs_2_, ...), custom_call_target="tpu_custom_call" | custom-call | bytes 3407872 | tf_op jit(solution)/shard_map/pallas_call | solution.py:282
  19.4 5.3 %all-to-all-start = ((f32[32,8,384]{2,1,0:T(8,128)}), f32[32,8,384]{2,1,0:T(8,128)S(1)}, u32[]{:S(2)}, u32[]{:S(2)}) async-start(f32[32,8,384]{2,1,0:T(8,128)} %bitcast.5), calls=%async_computation | async-start | bytes 786432 | tf_op jit(solution)/shard_map/all_to_all | solution.py:843
  24.7 0.0 copy-start.1
  24.8 1.8 %collective-permute-start.11 = (f32[3,64,256]{2,1,0:T(8,128)S(1)}, f32[3,64,256]{2,1,0:T(8,128)S(1)}, u32[]{:S(2)}, u32[]{:S(2)}) collective-permute-start(f32[3,64,256]{2,1,0:T(8,128)S(1)} %bitcast.14), channel_id=1, source_target_pairs={{0,16},{8,24},{16,0},{24,8},{1,17},{9,25},{17,1},{25,9},{2,18},{10... | collective-permute-start | bytes 589832 | tf_op jit(solution)/shard_map/ppermute | solution.py:788
  26.6 0.0 collective-permute-start.12
  26.6 1.5 %collective-permute-start = (bf16[2,256,256]{2,1,0:T(8,128)(2,1)}, bf16[2,256,256]{2,1,0:T(8,128)(2,1)S(1)}, u32[]{:S(2)}, u32[]{:S(2)}) collective-permute-start(bf16[2,256,256]{2,1,0:T(8,128)(2,1)} %get-tuple-element.16), channel_id=1, source_target_pairs={{0,1},{1,0},{2,3},{3,2},{4,5},{5,4},{6,7},{7,6},{8,9},{9,8},{10,11... | collective-permute-start | bytes 786440 | tf_op jit(solution)/shard_map/ppermute | solution.py:788
  28.1 3.4 %collective-permute-start.8 = (bf16[2,256,256]{2,1,0:T(8,128)(2,1)}, bf16[2,256,256]{2,1,0:T(8,128)(2,1)}, u32[]{:S(2)}, u32[]{:S(2)}) collective-permute-start(bf16[2,256,256]{2,1,0:T(8,128)(2,1)} %get-tuple-element.23), channel_id=1, source_target_pairs={{2,0},{7,1},{4,2},{1,3},{6,4},{3,5},{0,6},{5,7},{10,8},{15,9},{12,... | collective-permute-start | bytes 786440 | tf_op jit(solution)/shard_map/ppermute | solution.py:835
  31.4 0.0 collective-permute-start.7
  31.4 3.9 %collective-permute-done.11.refs_5_ = f32[3,64,256]{2,1,0:T(8,128)S(1)} collective-permute-done((f32[3,64,256]{2,1,0:T(8,128)S(1)}, f32[3,64,256]{2,1,0:T(8,128)S(1)}, u32[]{:S(2)}, u32[]{:S(2)}) %collective-permute-start.11) | collective-permute-done | bytes 196640 | tf_op jit(solution)/shard_map/ppermute | solution.py:788
  35.3 1.5 %collective-permute-start.6 = (bf16[2,256,256]{2,1,0:T(8,128)(2,1)}, bf16[2,256,256]{2,1,0:T(8,128)(2,1)S(1)}, u32[]{:S(2)}, u32[]{:S(2)}) collective-permute-start(bf16[2,256,256]{2,1,0:T(8,128)(2,1)} %get-tuple-element.23), channel_id=1, source_target_pairs={{0,1},{1,0},{2,3},{3,2},{4,5},{5,4},{6,7},{7,6},{8,9},{9,8},{10,11... | collective-permute-start | bytes 786440 | tf_op jit(solution)/shard_map/ppermute | solution.py:788
  36.8 0.0 collective-permute-done.12.refs_6_
  36.8 0.0 copy-start.3
  36.8 0.7 copy-done.3
  37.5 0.6 collective-permute-start.14
  38.1 0.1 collective-permute-done.close
  38.2 0.1 collective-permute-start.13
  38.3 5.5 %all-to-all-done.source = f32[32,8,384]{2,1,0:T(8,128)S(1)} async-done(((f32[32,8,384]{2,1,0:T(8,128)}), f32[32,8,384]{2,1,0:T(8,128)S(1)}, u32[]{:S(2)}, u32[]{:S(2)}) %all-to-all-start) | async-done | bytes 393248 | tf_op jit(solution)/shard_map/all_to_all | solution.py:843
  43.8 1.6 %shard_map.61 = f32[32,4,384]{2,1,0:T(4,128)} custom-call(s32[1]{0:T(128)} %bitcast.index, f32[32,8,384]{2,1,0:T(8,128)S(1)} %all-to-all-done.source, bf16[4,256,256]{2,1,0:T(8,128)(2,1)S(1)} %copy-done), custom_call_target="tpu_custom_call" | custom-call | bytes 1507328 | tf_op jit(solution)/shard_map/pallas_call | solution.py:282
  45.4 0.0 copy-start.4
  45.4 0.0 copy-start.5
  45.4 2.7 %all-to-all-start.1 = ((f32[32,4,384]{2,1,0:T(4,128)}), f32[32,4,384]{2,1,0:T(4,128)S(1)}, u32[]{:S(2)}, u32[]{:S(2)}) async-start(f32[32,4,384]{2,1,0:T(4,128)} %shard_map.61), calls=%async_computation.1 | async-start | bytes 393216 | tf_op jit(solution)/shard_map/all_to_all | solution.py:866
  48.1 0.0 collective-permute-done.8
  48.1 1.7 %collective-permute-start.9 = (bf16[2,256,256]{2,1,0:T(8,128)(2,1)}, bf16[2,256,256]{2,1,0:T(8,128)(2,1)S(1)}, u32[]{:S(2)}, u32[]{:S(2)}) collective-permute-start(bf16[2,256,256]{2,1,0:T(8,128)(2,1)} %collective-permute-done.8), channel_id=1, source_target_pairs={{0,1},{1,0},{2,3},{3,2},{4,5},{5,4},{6,7},{7,6},{8,9},{9,8},{10,11... | collective-permute-start | bytes 786440 | tf_op jit(solution)/shard_map/ppermute | solution.py:788
  49.8 0.0 collective-permute-done.7.refs_1_
  49.8 1.5 %collective-permute-start.10 = (bf16[2,256,256]{2,1,0:T(8,128)(2,1)S(1)}, bf16[2,256,256]{2,1,0:T(8,128)(2,1)S(1)}, u32[]{:S(2)}, u32[]{:S(2)}) collective-permute-start(bf16[2,256,256]{2,1,0:T(8,128)(2,1)S(1)} %collective-permute-done.7.refs_1_), channel_id=1, source_target_pairs={{0,2},{1,7},{2,4},{3,1},{4,6},{5,3},{6,0},{7,5},{8,10},{9,15},{10,... | collective-permute-start | bytes 786440 | tf_op jit(solution)/shard_map/ppermute | solution.py:837
  51.3 0.0 collective-permute-done.6.refs_0_
  51.3 0.0 collective-permute-start.15
  51.3 0.0 collective-permute-done.14.refs_9_
  51.4 0.5 collective-permute-start.16
  51.9 0.0 collective-permute-done.13.refs_7_
  51.9 1.5 %collective-permute-start.17 = (bf16[2,256,256]{2,1,0:T(8,128)(2,1)S(1)}, bf16[2,256,256]{2,1,0:T(8,128)(2,1)S(1)}, u32[]{:S(2)}, u32[]{:S(2)}) collective-permute-start(bf16[2,256,256]{2,1,0:T(8,128)(2,1)S(1)} %collective-permute-done.close), channel_id=1, source_target_pairs={{0,2},{1,7},{2,4},{3,1},{4,6},{5,3},{6,0},{7,5},{8,10},{9,15},{10,... | collective-permute-start | bytes 786440 | tf_op jit(solution)/shard_map/ppermute | solution.py:851
  53.4 5.3 %collective-permute-done.9.refs_2_ = bf16[2,256,256]{2,1,0:T(8,128)(2,1)S(1)} collective-permute-done((bf16[2,256,256]{2,1,0:T(8,128)(2,1)}, bf16[2,256,256]{2,1,0:T(8,128)(2,1)S(1)}, u32[]{:S(2)}, u32[]{:S(2)}) %collective-permute-start.9) | collective-permute-done | bytes 262176 | tf_op jit(solution)/shard_map/ppermute | solution.py:788
  58.7 3.4 %collective-permute-done.10.refs_3_ = bf16[2,256,256]{2,1,0:T(8,128)(2,1)S(1)} collective-permute-done((bf16[2,256,256]{2,1,0:T(8,128)(2,1)S(1)}, bf16[2,256,256]{2,1,0:T(8,128)(2,1)S(1)}, u32[]{:S(2)}, u32[]{:S(2)}) %collective-permute-start.10) | collective-permute-done | bytes 262176 | tf_op jit(solution)/shard_map/ppermute | solution.py:837
  62.1 0.0 collective-permute-done.15.refs_10_
  62.1 0.0 collective-permute-done.16.refs_11_
  62.1 0.0 copy-done.1
  62.1 0.0 copy-done.4
  62.1 0.0 copy-done.5
  62.1 4.2 %shard_map.63 = (bf16[2,3,256,256]{3,2,1,0:T(8,128)(2,1)}, f32[2,256,256]{2,1,0:T(8,128)S(1)}, f32[256,256]{1,0:T(8,128)S(1)}) custom-call(s32[1]{0:T(128)} %bitcast.1.index.spot, s32[1]{0:T(128)} %bitcast.4.signs, f32[2,3]{1,0:T(2,128)S(1)} %copy-done.5, bf16[2,3,256,256]{3,2,1,0:T(8,128)(2,1)S(1)} %bitcast.10, ...), custom_call_target="tpu_custom_call" | custom-call | flops 26214400 | bytes 7602176 | tf_op jit(solution)/shard_map/pallas_call | solution.py:282
  66.3 0.8 %collective-permute-done.17.remote = bf16[2,256,256]{2,1,0:T(8,128)(2,1)S(1)} collective-permute-done((bf16[2,256,256]{2,1,0:T(8,128)(2,1)S(1)}, bf16[2,256,256]{2,1,0:T(8,128)(2,1)S(1)}, u32[]{:S(2)}, u32[]{:S(2)}) %collective-permute-start.17) | collective-permute-done | bytes 262176 | tf_op jit(solution)/shard_map/ppermute | solution.py:851
  67.2 0.8 %shard_map.64 = bf16[2,3,256,256]{3,2,1,0:T(8,128)(2,1)} custom-call(f32[2,256,256]{2,1,0:T(8,128)S(1)} %get-tuple-element.26.partial, f32[256,256]{1,0:T(8,128)S(1)} %get-tuple-element.27.speed, bf16[2,256,256]{2,1,0:T(8,128)(2,1)S(1)} %collective-permute-done.close, ...), custom_call_target="tpu_custom_call", output_to_operand_aliasing={{}: (4, {})} | custom-call | flops 524288 | bytes 3145728 | tf_op jit(solution)/shard_map/pallas_call | solution.py:282
  68.0 0.0 all-to-all-done.1.source
  68.0 1.0 %shard_map.62 = f32[3,1,64,256]{3,2,1,0:T(8,128)} custom-call(f32[32,4,384]{2,1,0:T(4,128)S(1)} %all-to-all-done.1.source, bf16[4,256,256]{2,1,0:T(8,128)(2,1)S(1)} %copy-done), custom_call_target="tpu_custom_call" | custom-call | bytes 1114112 | tf_op jit(solution)/shard_map/pallas_call | solution.py:282
Async XLA Ops:
  0.6 17.2 %copy-start = (bf16[4,256,256]{2,1,0:T(8,128)(2,1)S(1)}, bf16[4,256,256]{2,1,0:T(8,128)(2,1)}, u32[]{:S(2)}) copy-start(bf16[4,256,256]{2,1,0:T(8,128)(2,1)} %constant.16.clone.refs_7_.tables) | copy-start | bytes 1572868
  0.6 9.0 %collective-permute-start.4 = (f32[3,64,256]{2,1,0:T(8,128)}, f32[3,64,256]{2,1,0:T(8,128)S(1)}, u32[]{:S(2)}, u32[]{:S(2)}) collective-permute-start(f32[3,64,256]{2,1,0:T(8,128)} %bitcast.11), channel_id=1, source_target_pairs={{0,1},{1,0},{2,3},{3,2},{4,5},{5,4},{6,7},{7,6},{8,9},{9,8},{10,11... | collective-permute-start | bytes 589832 | tf_op jit(solution)/shard_map/ppermute | solution.py:788
  3.7 14.1 %copy-start.2 = (f32[3,1,64,256]{3,2,1,0:T(8,128)S(1)}, f32[3,1,64,256]{3,2,1,0:T(8,128)}, u32[]{:S(2)}) copy-start(f32[3,1,64,256]{3,2,1,0:T(8,128)} %param.4) | copy-start | bytes 589828
  6.6 6.9 %collective-permute-start.1 = (bf16[416,256]{1,0:T(8,128)(2,1)S(1)}, bf16[416,256]{1,0:T(8,128)(2,1)S(1)}, u32[]{:S(2)}, u32[]{:S(2)}) collective-permute-start(bf16[416,256]{1,0:T(8,128)(2,1)S(1)} %get-tuple-element.18), channel_id=1, source_target_pairs={{0,8},{8,16},{16,24},{24,0},{1,9},{9,17},{17,25},{25,1},{2,10},{10... | collective-permute-start | bytes 638984 | tf_op jit(solution)/shard_map/ppermute | solution.py:783
  6.7 8.2 %collective-permute-start.2 = (bf16[416,256]{1,0:T(8,128)(2,1)S(1)}, bf16[416,256]{1,0:T(8,128)(2,1)S(1)}, u32[]{:S(2)}, u32[]{:S(2)}) collective-permute-start(bf16[416,256]{1,0:T(8,128)(2,1)S(1)} %get-tuple-element.19), channel_id=1, source_target_pairs={{0,16},{8,24},{16,0},{24,8},{1,17},{9,25},{17,1},{25,9},{2,18},{10... | collective-permute-start | bytes 638984 | tf_op jit(solution)/shard_map/ppermute | solution.py:783
  8.2 9.6 %collective-permute-start.3 = (bf16[416,256]{1,0:T(8,128)(2,1)S(1)}, bf16[416,256]{1,0:T(8,128)(2,1)S(1)}, u32[]{:S(2)}, u32[]{:S(2)}) collective-permute-start(bf16[416,256]{1,0:T(8,128)(2,1)S(1)} %get-tuple-element.20), channel_id=1, source_target_pairs={{0,24},{8,0},{16,8},{24,16},{1,25},{9,1},{17,9},{25,17},{2,26},{10... | collective-permute-start | bytes 638984 | tf_op jit(solution)/shard_map/ppermute | solution.py:783
  9.6 8.2 %collective-permute-start.5 = (f32[3,64,256]{2,1,0:T(8,128)S(1)}, f32[3,64,256]{2,1,0:T(8,128)S(1)}, u32[]{:S(2)}, u32[]{:S(2)}) collective-permute-start(f32[3,64,256]{2,1,0:T(8,128)S(1)} %collective-permute-done.4.refs_5_), channel_id=1, source_target_pairs={{0,2},{1,7},{2,4},{3,1},{4,6},{5,3},{6,0},{7,5},{8,10},{9,15},{10,... | collective-permute-start | bytes 589832 | tf_op jit(solution)/shard_map/ppermute | solution.py:830
  19.4 24.4 %all-to-all-start = ((f32[32,8,384]{2,1,0:T(8,128)}), f32[32,8,384]{2,1,0:T(8,128)S(1)}, u32[]{:S(2)}, u32[]{:S(2)}) async-start(f32[32,8,384]{2,1,0:T(8,128)} %bitcast.5), calls=%async_computation | async-start | bytes 786432 | tf_op jit(solution)/shard_map/all_to_all | solution.py:843
  24.7 37.4 %copy-start.1 = (bf16[2,3,1,256,256]{4,3,2,1,0:T(8,128)(2,1)S(1)}, bf16[2,3,1,256,256]{4,3,2,1,0:T(8,128)(2,1)}, u32[]{:S(2)}) copy-start(bf16[2,3,1,256,256]{4,3,2,1,0:T(8,128)(2,1)} %param.5) | copy-start | bytes 2359300
  24.8 10.6 %collective-permute-start.11 = (f32[3,64,256]{2,1,0:T(8,128)S(1)}, f32[3,64,256]{2,1,0:T(8,128)S(1)}, u32[]{:S(2)}, u32[]{:S(2)}) collective-permute-start(f32[3,64,256]{2,1,0:T(8,128)S(1)} %bitcast.14), channel_id=1, source_target_pairs={{0,16},{8,24},{16,0},{24,8},{1,17},{9,25},{17,1},{25,9},{2,18},{10... | collective-permute-start | bytes 589832 | tf_op jit(solution)/shard_map/ppermute | solution.py:788
  26.6 10.2 %collective-permute-start.12 = (f32[3,64,256]{2,1,0:T(8,128)S(1)}, f32[3,64,256]{2,1,0:T(8,128)S(1)}, u32[]{:S(2)}, u32[]{:S(2)}) collective-permute-start(f32[3,64,256]{2,1,0:T(8,128)S(1)} %bitcast.15), channel_id=1, source_target_pairs={{0,8},{8,0},{16,24},{24,16},{1,9},{9,1},{17,25},{25,17},{2,10},{10... | collective-permute-start | bytes 589832 | tf_op jit(solution)/shard_map/ppermute | solution.py:788
  26.6 11.6 %collective-permute-start = (bf16[2,256,256]{2,1,0:T(8,128)(2,1)}, bf16[2,256,256]{2,1,0:T(8,128)(2,1)S(1)}, u32[]{:S(2)}, u32[]{:S(2)}) collective-permute-start(bf16[2,256,256]{2,1,0:T(8,128)(2,1)} %get-tuple-element.16), channel_id=1, source_target_pairs={{0,1},{1,0},{2,3},{3,2},{4,5},{5,4},{6,7},{7,6},{8,9},{9,8},{10,11... | collective-permute-start | bytes 786440 | tf_op jit(solution)/shard_map/ppermute | solution.py:788
  28.1 20.0 %collective-permute-start.8 = (bf16[2,256,256]{2,1,0:T(8,128)(2,1)}, bf16[2,256,256]{2,1,0:T(8,128)(2,1)}, u32[]{:S(2)}, u32[]{:S(2)}) collective-permute-start(bf16[2,256,256]{2,1,0:T(8,128)(2,1)} %get-tuple-element.23), channel_id=1, source_target_pairs={{2,0},{7,1},{4,2},{1,3},{6,4},{3,5},{0,6},{5,7},{10,8},{15,9},{12,... | collective-permute-start | bytes 786440 | tf_op jit(solution)/shard_map/ppermute | solution.py:835
  31.4 18.4 %collective-permute-start.7 = (bf16[2,256,256]{2,1,0:T(8,128)(2,1)}, bf16[2,256,256]{2,1,0:T(8,128)(2,1)S(1)}, u32[]{:S(2)}, u32[]{:S(2)}) collective-permute-start(bf16[2,256,256]{2,1,0:T(8,128)(2,1)} %get-tuple-element.24), channel_id=1, source_target_pairs={{0,1},{1,0},{2,3},{3,2},{4,5},{5,4},{6,7},{7,6},{8,9},{9,8},{10,11... | collective-permute-start | bytes 786440 | tf_op jit(solution)/shard_map/ppermute | solution.py:788
  35.3 16.0 %collective-permute-start.6 = (bf16[2,256,256]{2,1,0:T(8,128)(2,1)}, bf16[2,256,256]{2,1,0:T(8,128)(2,1)S(1)}, u32[]{:S(2)}, u32[]{:S(2)}) collective-permute-start(bf16[2,256,256]{2,1,0:T(8,128)(2,1)} %get-tuple-element.23), channel_id=1, source_target_pairs={{0,1},{1,0},{2,3},{3,2},{4,5},{5,4},{6,7},{7,6},{8,9},{9,8},{10,11... | collective-permute-start | bytes 786440 | tf_op jit(solution)/shard_map/ppermute | solution.py:788
  36.8 0.7 copy-start.3
  37.5 13.9 %collective-permute-start.14 = (f32[4,64,256]{2,1,0:T(8,128)S(1)}, f32[4,64,256]{2,1,0:T(8,128)S(1)}, u32[]{:S(2)}, u32[]{:S(2)}) collective-permute-start(f32[4,64,256]{2,1,0:T(8,128)S(1)} %get-tuple-element.25.refs_8_), channel_id=1, source_target_pairs={{0,16},{8,24},{16,0},{24,8},{1,17},{9,25},{17,1},{25,9},{2,18},{10... | collective-permute-start | bytes 786440 | tf_op jit(solution)/shard_map/ppermute | solution.py:788
  38.2 13.7 %collective-permute-start.13 = (f32[3,64,256]{2,1,0:T(8,128)S(1)}, f32[3,64,256]{2,1,0:T(8,128)}, u32[]{:S(2)}, u32[]{:S(2)}) collective-permute-start(f32[3,64,256]{2,1,0:T(8,128)S(1)} %collective-permute-done.11.refs_5_), channel_id=1, source_target_pairs={{0,8},{8,0},{16,24},{24,16},{1,9},{9,1},{17,25},{25,17},{2,10},{10... | collective-permute-start | bytes 589832 | tf_op jit(solution)/shard_map/ppermute | solution.py:788
  45.4 16.8 %copy-start.4 = (f32[3,64,256]{2,1,0:T(8,128)S(1)}, f32[3,64,256]{2,1,0:T(8,128)}, u32[]{:S(2)}) copy-start(f32[3,64,256]{2,1,0:T(8,128)} %copy-done.3) | copy-start | bytes 589828
  45.4 16.8 %copy-start.5 = (f32[2,3]{1,0:T(2,128)S(1)}, f32[2,3]{1,0:T(2,128)}, u32[]{:S(2)}) copy-start(f32[2,3]{1,0:T(2,128)} %kick.1) | copy-start | bytes 76
  45.4 22.7 %all-to-all-start.1 = ((f32[32,4,384]{2,1,0:T(4,128)}), f32[32,4,384]{2,1,0:T(4,128)S(1)}, u32[]{:S(2)}, u32[]{:S(2)}) async-start(f32[32,4,384]{2,1,0:T(4,128)} %shard_map.61), calls=%async_computation.1 | async-start | bytes 393216 | tf_op jit(solution)/shard_map/all_to_all | solution.py:866
  48.1 10.6 %collective-permute-start.9 = (bf16[2,256,256]{2,1,0:T(8,128)(2,1)}, bf16[2,256,256]{2,1,0:T(8,128)(2,1)S(1)}, u32[]{:S(2)}, u32[]{:S(2)}) collective-permute-start(bf16[2,256,256]{2,1,0:T(8,128)(2,1)} %collective-permute-done.8), channel_id=1, source_target_pairs={{0,1},{1,0},{2,3},{3,2},{4,5},{5,4},{6,7},{7,6},{8,9},{9,8},{10,11... | collective-permute-start | bytes 786440 | tf_op jit(solution)/shard_map/ppermute | solution.py:788
  49.8 12.3 %collective-permute-start.10 = (bf16[2,256,256]{2,1,0:T(8,128)(2,1)S(1)}, bf16[2,256,256]{2,1,0:T(8,128)(2,1)S(1)}, u32[]{:S(2)}, u32[]{:S(2)}) collective-permute-start(bf16[2,256,256]{2,1,0:T(8,128)(2,1)S(1)} %collective-permute-done.7.refs_1_), channel_id=1, source_target_pairs={{0,2},{1,7},{2,4},{3,1},{4,6},{5,3},{6,0},{7,5},{8,10},{9,15},{10,... | collective-permute-start | bytes 786440 | tf_op jit(solution)/shard_map/ppermute | solution.py:837
  51.3 10.8 %collective-permute-start.15 = (f32[4,64,256]{2,1,0:T(8,128)S(1)}, f32[4,64,256]{2,1,0:T(8,128)S(1)}, u32[]{:S(2)}, u32[]{:S(2)}) collective-permute-start(f32[4,64,256]{2,1,0:T(8,128)S(1)} %get-tuple-element.25.refs_8_), channel_id=1, source_target_pairs={{0,8},{8,0},{16,24},{24,16},{1,9},{9,1},{17,25},{25,17},{2,10},{10... | collective-permute-start | bytes 786440 | tf_op jit(solution)/shard_map/ppermute | solution.py:788
  51.4 10.8 %collective-permute-start.16 = (f32[4,64,256]{2,1,0:T(8,128)S(1)}, f32[4,64,256]{2,1,0:T(8,128)S(1)}, u32[]{:S(2)}, u32[]{:S(2)}) collective-permute-start(f32[4,64,256]{2,1,0:T(8,128)S(1)} %collective-permute-done.14.refs_9_), channel_id=1, source_target_pairs={{0,8},{8,0},{16,24},{24,16},{1,9},{9,1},{17,25},{25,17},{2,10},{10... | collective-permute-start | bytes 786440 | tf_op jit(solution)/shard_map/ppermute | solution.py:788
  51.9 15.3 %collective-permute-start.17 = (bf16[2,256,256]{2,1,0:T(8,128)(2,1)S(1)}, bf16[2,256,256]{2,1,0:T(8,128)(2,1)S(1)}, u32[]{:S(2)}, u32[]{:S(2)}) collective-permute-start(bf16[2,256,256]{2,1,0:T(8,128)(2,1)S(1)} %collective-permute-done.close), channel_id=1, source_target_pairs={{0,2},{1,7},{2,4},{3,1},{4,6},{5,3},{6,0},{7,5},{8,10},{9,15},{10,... | collective-permute-start | bytes 786440 | tf_op jit(solution)/shard_map/ppermute | solution.py:851

commit v3 on v2

--- a/solution.py
+++ b/solution.py
@@ -264,6 +264,7 @@
 
 
 def run_kernel(body, outs, args, scalars=(), scratch=(), flops=0, far=(), far_outs=(), aliases=None):
+    outs = list(outs) if isinstance(outs, list) else outs
     leaves = list(args) + jax.tree.leaves(outs)
     leaves += [leaf for leaf in scratch if leaf.memory_space == pltpu.VMEM]
     held = sum(math.prod(leaf.shape) * jnp.dtype(leaf.dtype).itemsize for leaf in leaves)
@@ -274,6 +275,7 @@
     spaces = jax.tree.map(lambda _: pl.BlockSpec(memory_space=pltpu.VMEM), outs)
     for number in far_outs:
         spaces[number] = pl.BlockSpec(memory_space=pltpu.HBM)
+        outs[number] = pltpu.HBM(outs[number].shape, outs[number].dtype)
     in_specs = [pl.BlockSpec(memory_space=pltpu.SMEM) for _ in scalars]
     in_specs += [
         pl.BlockSpec(memory_space=pltpu.HBM if number in far else pltpu.VMEM)
@@ -304,46 +306,50 @@
 
     def pack(index, source, motion, *refs):
         targets, singles = refs[:groups], refs[groups : groups + dims]
-        edges, ends, copied, fetched, ended, alone = refs[groups + dims :]
+        held, ends, rims, fetched, ended, copied, alone, placed = refs[groups + dims :]
         last = motion.shape[1] - END_ROWS
-        moves = [
+        tips = [
             pltpu.make_async_copy(
                 motion.at[:, first : first + END_ROWS, :], ends.at[side], ended.at[side]
             )
             for side, first in enumerate((0, last))
         ]
-        for shift in range(groups):
-            block = (index[0] + shift) % groups
-            start = pl.multiple_of(block * rows, rows)
-            above = pl.multiple_of((block + groups - 1) % groups * rows + rows - ROW_TILE, ROW_TILE)
-            below = pl.multiple_of((block + 1) % groups * rows, rows)
-            for side, place in enumerate((above, below)):
-                moves.append(
-                    pltpu.make_async_copy(
-                        source.at[:, :, pl.ds(place, ROW_TILE), :],
-                        edges.at[shift, side],
-                        fetched.at[shift, side],
-                    )
-                )
-            for plane in range(planes):
-                moves.append(
-                    pltpu.make_async_copy(
-                        source.at[plane // dims, plane % dims, pl.ds(start, rows), :],
-                        targets[shift].at[plane * rows : (plane + 1) * rows, :],
-                        copied.at[shift, plane],
-                    )
-                )
-        lone = [
-            pltpu.make_async_copy(source.at[:, dim], singles[dim], alone.at[dim])
+        loads = [
+            pltpu.make_async_copy(source.at[:, dim], held.at[dim], fetched.at[dim])
             for dim in range(dims)
         ]
-        for move in moves + lone:
+        for move in loads + tips:
             move.start()
+        blocks = [(index[0] + shift) % groups for shift in range(groups)]
+        moves = []
+        for dim in range(dims):
+            loads[dim].wait()
+            for shift in range(1, groups):
+                start = pl.multiple_of(blocks[shift] * rows, rows)
+                for member in range(members):
+                    plane = member * dims + dim
+                    moves.append(
+                        pltpu.make_async_copy(
+                            held.at[dim, member, pl.ds(start, rows), :],
+                            targets[shift].at[plane * rows : (plane + 1) * rows, :],
+                            copied.at[shift, plane],
+                        )
+                    )
+                    moves[-1].start()
+            moves.append(pltpu.make_async_copy(held.at[dim], singles[dim], alone.at[dim]))
+            moves[-1].start()
+        start = pl.multiple_of(blocks[0] * rows, rows)
+        for dim in range(dims):
+            for member in range(members):
+                plane = member * dims + dim
+                targets[0][plane * rows : (plane + 1) * rows, :] = held[
+                    dim, member, pl.ds(start, rows), :
+                ]
+        for move in tips:
+            move.wait()
         place = row_index((rim, size_y))
         common = jnp.zeros((rim, size_y), jnp.float32)
         slot = 2 * planes
-        for move in moves[:2]:
-            move.wait()
         for side, line in enumerate((0, END_ROWS - 1)):
             for dim in range(dims):
                 rest = ends[side, dim][line : line + 1, :]
@@ -352,21 +358,35 @@
                     rest = rest - part
                     common = jnp.where(place == slot, part, common)
                     slot += 1
-        for move in moves[2:]:
-            move.wait()
         for shift in range(groups):
+            above = pl.multiple_of(
+                (blocks[shift] + groups - 1) % groups * rows + rows - ROW_TILE, ROW_TILE
+            )
+            below = pl.multiple_of((blocks[shift] + 1) % groups * rows, rows)
             edge = common
             for member in range(members):
                 for dim in range(dims):
-                    top = edges[shift, 0, member, dim].astype(jnp.float32)
-                    bottom = edges[shift, 1, member, dim].astype(jnp.float32)
+                    top = held[dim, member, pl.ds(above, ROW_TILE), :].astype(jnp.float32)
+                    bottom = held[dim, member, pl.ds(below, ROW_TILE), :].astype(jnp.float32)
                     slot = dim * 2 * members + member * 2
                     edge = jnp.where(place == slot, top[ROW_TILE - 1 :], edge)
                     edge = jnp.where(place == slot + 1, bottom[:1], edge)
-            targets[shift][planes * rows :, :] = edge.astype(fields.dtype)
-        for move in lone:
+            if shift == 0:
+                targets[0][planes * rows :, :] = edge.astype(fields.dtype)
+                continue
+            rims[shift] = edge.astype(fields.dtype)
+            moves.append(
+                pltpu.make_async_copy(
+                    rims.at[shift],
+                    targets[shift].at[planes * rows : planes * rows + rim, :],
+                    placed.at[shift],
+                )
+            )
+            moves[-1].start()
+        for move in moves:
             move.wait()
 
+    count = groups + dims
     return run_kernel(
         pack,
         [shape] * groups
@@ -374,14 +394,17 @@
         [fields, flow],
         [grp_index],
         scratch=[
-            pltpu.VMEM((groups, 2, members, dims, ROW_TILE, size_y), fields.dtype),
+            pltpu.VMEM((dims, members, size_x, size_y), fields.dtype),
             pltpu.VMEM((2, 3, END_ROWS, size_y), flow.dtype),
+            pltpu.VMEM((groups, rim, size_y), fields.dtype),
+            pltpu.SemaphoreType.DMA((dims,)),
+            pltpu.SemaphoreType.DMA((2,)),
             pltpu.SemaphoreType.DMA((groups, planes)),
-            pltpu.SemaphoreType.DMA((groups, 2)),
-            pltpu.SemaphoreType.DMA((2,)),
             pltpu.SemaphoreType.DMA((dims,)),
+            pltpu.SemaphoreType.DMA((groups,)),
         ],
         far=(0, 1),
+        far_outs=range(1, count),
     )
 
 

time: 69.3 us -> 69 us (level)
  transfers between devices with their start and end apart: 20 -> 20, of which waited for: 9 -> 9; matrix products, arithmetic and copies ran while one was open for 0% -> 0% of each run, Pallas kernels for 14% -> 13%
where the time goes in v3:
time: 69 us; the launch traced here: 68.7 us
  starting transfers between devices  29.7 us (43%)
  waiting for transfers between devices  25.9 us (38%)
  Pallas kernels  11.6 us (17%)
  between operations  0.75 us (1%)
  local copies, waits for them, and re-layouts  0.7 us (1%)
    pallas_call x6, Pallas kernels, run_kernel(): pl.pallas_call(body, out_shape=outs, in_specs=in_specs, out_specs=spaces,...  11.6 us
    ppermute x11, starting transfers between devices, flipped(): return lax.ppermute(value, axis, [(i, i ^ bit) for i in range(count)])  10.8 us
    ppermute x11, waiting for transfers between devices, flipped(): return lax.ppermute(value, axis, [(i, i ^ bit) for i in range(count)])  9.3 us
    ppermute x3, waiting for transfers between devices, shifted(): lax.ppermute(value, axis, [(i, (i + step) % count) for i in range(count)])  6.9 us
    all_to_all x1, waiting for transfers between devices, pencil_shards(): lax.all_to_all(spectra.reshape(devices, block, 6 * rows), ('grp', 'slab')...  5.46 us
    all_to_all x1, starting transfers between devices, pencil_shards(): lax.all_to_all(spectra.reshape(devices, block, 6 * rows), ('grp', 'slab')...  5.21 us
    ppermute x1, waiting for transfers between devices, pencil_shards(): far.append(lax.ppermute(near[1], 'slab', two_up))  3.45 us
    ppermute x1, starting transfers between devices, pencil_shards(): hopped = lax.ppermute(parts[0], 'slab', two_down)  3.36 us
  transfers between devices with their start and end apart: 20, of which 9 were waited for; matrix products, arithmetic and copies ran while one was open for 0% of the time, Pallas kernels for 13%

profile of v3, /device:TPU:0, one launch (start us, length us, event | category | flops | bytes accessed | tf_op | source)
XLA Modules:
  0.0 68.7 jit_solution(4036898573374387265)
XLA Ops:
  0.6 0.0 copy-start
  0.6 3.1 %collective-permute-start.4 = (f32[3,64,256]{2,1,0:T(8,128)}, f32[3,64,256]{2,1,0:T(8,128)S(1)}, u32[]{:S(2)}, u32[]{:S(2)}) collective-permute-start(f32[3,64,256]{2,1,0:T(8,128)} %bitcast.11), channel_id=1, source_target_pairs={{0,1},{1,0},{2,3},{3,2},{4,5},{5,4},{6,7},{7,6},{8,9},{9,8},{10,11... | collective-permute-start | bytes 589832 | tf_op jit(solution)/shard_map/ppermute | solution.py:811
  3.7 0.0 copy-start.2
  3.7 2.4 %shard_map.59 = (bf16[416,256]{1,0:T(8,128)(2,1)S(1)}, bf16[416,256]{1,0:T(8,128)(2,1)}, bf16[416,256]{1,0:T(8,128)(2,1)}, bf16[416,256]{1,0:T(8,128)(2,1)}, bf1...) custom-call(s32[1]{0:T(128)} %bitcast.1.index.spot, ...), custom_call_target="tpu_custom_call" | custom-call | bytes 3522560 | tf_op jit(solution)/shard_map/pallas_call | solution.py:284
  6.1 0.1 collective-permute-start.1
  6.2 1.6 %collective-permute-start.2 = (bf16[416,256]{1,0:T(8,128)(2,1)}, bf16[416,256]{1,0:T(8,128)(2,1)S(1)}, u32[]{:S(2)}, u32[]{:S(2)}) collective-permute-start(bf16[416,256]{1,0:T(8,128)(2,1)} %get-tuple-element.19), channel_id=1, source_target_pairs={{0,16},{8,24},{16,0},{24,8},{1,17},{9,25},{17,1},{25,9},{2,18},{10... | collective-permute-start | bytes 638984 | tf_op jit(solution)/shard_map/ppermute | solution.py:806
  7.7 1.4 %collective-permute-start.3 = (bf16[416,256]{1,0:T(8,128)(2,1)}, bf16[416,256]{1,0:T(8,128)(2,1)S(1)}, u32[]{:S(2)}, u32[]{:S(2)}) collective-permute-start(bf16[416,256]{1,0:T(8,128)(2,1)} %get-tuple-element.20), channel_id=1, source_target_pairs={{0,24},{8,0},{16,8},{24,16},{1,25},{9,1},{17,9},{25,17},{2,26},{10... | collective-permute-start | bytes 638984 | tf_op jit(solution)/shard_map/ppermute | solution.py:806
  9.1 0.0 collective-permute-done.4.refs_5_
  9.1 1.6 %collective-permute-start.5 = (f32[3,64,256]{2,1,0:T(8,128)S(1)}, f32[3,64,256]{2,1,0:T(8,128)S(1)}, u32[]{:S(2)}, u32[]{:S(2)}) collective-permute-start(f32[3,64,256]{2,1,0:T(8,128)S(1)} %collective-permute-done.4.refs_5_), channel_id=1, source_target_pairs={{0,2},{1,7},{2,4},{3,1},{4,6},{5,3},{6,0},{7,5},{8,10},{9,15},{10,... | collective-permute-start | bytes 589832 | tf_op jit(solution)/shard_map/ppermute | solution.py:853
  10.7 2.6 %collective-permute-done.1.refs_1_ = bf16[416,256]{1,0:T(8,128)(2,1)S(1)} collective-permute-done((bf16[416,256]{1,0:T(8,128)(2,1)}, bf16[416,256]{1,0:T(8,128)(2,1)S(1)}, u32[]{:S(2)}, u32[]{:S(2)}) %collective-permute-start.1) | collective-permute-done | bytes 213024 | tf_op jit(solution)/shard_map/ppermute | solution.py:806
  13.3 1.3 %collective-permute-done.2.refs_2_ = bf16[416,256]{1,0:T(8,128)(2,1)S(1)} collective-permute-done((bf16[416,256]{1,0:T(8,128)(2,1)}, bf16[416,256]{1,0:T(8,128)(2,1)S(1)}, u32[]{:S(2)}, u32[]{:S(2)}) %collective-permute-start.2) | collective-permute-done | bytes 213024 | tf_op jit(solution)/shard_map/ppermute | solution.py:806
  14.6 3.0 %collective-permute-done.3.refs_3_ = bf16[416,256]{1,0:T(8,128)(2,1)S(1)} collective-permute-done((bf16[416,256]{1,0:T(8,128)(2,1)}, bf16[416,256]{1,0:T(8,128)(2,1)S(1)}, u32[]{:S(2)}, u32[]{:S(2)}) %collective-permute-start.3) | collective-permute-done | bytes 213024 | tf_op jit(solution)/shard_map/ppermute | solution.py:806
  17.6 0.0 collective-permute-done.5.refs_6_
  17.6 0.0 copy-done
  17.6 0.0 copy-done.2
  17.6 1.6 %shard_map.60 = (f32[256,384]{1,0:T(8,128)}, f32[4,64,256]{2,1,0:T(8,128)S(1)}) custom-call(s32[1]{0:T(128)} %bitcast.4.signs, bf16[416,256]{1,0:T(8,128)(2,1)S(1)} %get-tuple-element.17.refs_0_, bf16[416,256]{1,0:T(8,128)(2,1)S(1)} %collective-permute-done.1.refs_1_, bf16[416,256]{1,0:T(8,128)(2,1)S(1)} %collective-permute-done.2.refs_2_, ...), custom_call_target="tpu_custom_call" | custom-call | bytes 3407872 | tf_op jit(solution)/shard_map/pallas_call | solution.py:284
  19.2 5.2 %all-to-all-start = ((f32[32,8,384]{2,1,0:T(8,128)}), f32[32,8,384]{2,1,0:T(8,128)S(1)}, u32[]{:S(2)}, u32[]{:S(2)}) async-start(f32[32,8,384]{2,1,0:T(8,128)} %bitcast.5), calls=%async_computation | async-start | bytes 786432 | tf_op jit(solution)/shard_map/all_to_all | solution.py:866
  24.4 0.0 copy-start.1
  24.4 1.8 %collective-permute-start.11 = (f32[3,64,256]{2,1,0:T(8,128)S(1)}, f32[3,64,256]{2,1,0:T(8,128)S(1)}, u32[]{:S(2)}, u32[]{:S(2)}) collective-permute-start(f32[3,64,256]{2,1,0:T(8,128)S(1)} %bitcast.14), channel_id=1, source_target_pairs={{0,16},{8,24},{16,0},{24,8},{1,17},{9,25},{17,1},{25,9},{2,18},{10... | collective-permute-start | bytes 589832 | tf_op jit(solution)/shard_map/ppermute | solution.py:811
  26.3 0.0 collective-permute-start.12
  26.3 1.5 %collective-permute-start = (bf16[2,256,256]{2,1,0:T(8,128)(2,1)}, bf16[2,256,256]{2,1,0:T(8,128)(2,1)S(1)}, u32[]{:S(2)}, u32[]{:S(2)}) collective-permute-start(bf16[2,256,256]{2,1,0:T(8,128)(2,1)} %get-tuple-element.16), channel_id=1, source_target_pairs={{0,1},{1,0},{2,3},{3,2},{4,5},{5,4},{6,7},{7,6},{8,9},{9,8},{10,11... | collective-permute-start | bytes 786440 | tf_op jit(solution)/shard_map/ppermute | solution.py:811
  27.7 3.4 %collective-permute-start.8 = (bf16[2,256,256]{2,1,0:T(8,128)(2,1)}, bf16[2,256,256]{2,1,0:T(8,128)(2,1)}, u32[]{:S(2)}, u32[]{:S(2)}) collective-permute-start(bf16[2,256,256]{2,1,0:T(8,128)(2,1)} %get-tuple-element.23), channel_id=1, source_target_pairs={{2,0},{7,1},{4,2},{1,3},{6,4},{3,5},{0,6},{5,7},{10,8},{15,9},{12,... | collective-permute-start | bytes 786440 | tf_op jit(solution)/shard_map/ppermute | solution.py:858
  31.1 0.0 collective-permute-start.7
  31.1 3.9 %collective-permute-done.11.refs_5_ = f32[3,64,256]{2,1,0:T(8,128)S(1)} collective-permute-done((f32[3,64,256]{2,1,0:T(8,128)S(1)}, f32[3,64,256]{2,1,0:T(8,128)S(1)}, u32[]{:S(2)}, u32[]{:S(2)}) %collective-permute-start.11) | collective-permute-done | bytes 196640 | tf_op jit(solution)/shard_map/ppermute | solution.py:811
  35.0 1.5 %collective-permute-start.6 = (bf16[2,256,256]{2,1,0:T(8,128)(2,1)}, bf16[2,256,256]{2,1,0:T(8,128)(2,1)S(1)}, u32[]{:S(2)}, u32[]{:S(2)}) collective-permute-start(bf16[2,256,256]{2,1,0:T(8,128)(2,1)} %get-tuple-element.23), channel_id=1, source_target_pairs={{0,1},{1,0},{2,3},{3,2},{4,5},{5,4},{6,7},{7,6},{8,9},{9,8},{10,11... | collective-permute-start | bytes 786440 | tf_op jit(solution)/shard_map/ppermute | solution.py:811
  36.5 0.0 collective-permute-done.12.refs_6_
  36.5 0.0 copy-start.3
  36.5 0.7 copy-done.3
  37.2 0.6 collective-permute-start.14
  37.8 0.1 collective-permute-done.close
  37.9 0.1 collective-permute-start.13
  38.0 5.5 %all-to-all-done.source = f32[32,8,384]{2,1,0:T(8,128)S(1)} async-done(((f32[32,8,384]{2,1,0:T(8,128)}), f32[32,8,384]{2,1,0:T(8,128)S(1)}, u32[]{:S(2)}, u32[]{:S(2)}) %all-to-all-start) | async-done | bytes 393248 | tf_op jit(solution)/shard_map/all_to_all | solution.py:866
  43.5 1.6 %shard_map.61 = f32[32,4,384]{2,1,0:T(4,128)} custom-call(s32[1]{0:T(128)} %bitcast.index, f32[32,8,384]{2,1,0:T(8,128)S(1)} %all-to-all-done.source, bf16[4,256,256]{2,1,0:T(8,128)(2,1)S(1)} %copy-done), custom_call_target="tpu_custom_call" | custom-call | bytes 1507328 | tf_op jit(solution)/shard_map/pallas_call | solution.py:284
  45.0 0.0 copy-start.4
  45.0 0.0 copy-start.5
  45.1 2.7 %all-to-all-start.1 = ((f32[32,4,384]{2,1,0:T(4,128)}), f32[32,4,384]{2,1,0:T(4,128)S(1)}, u32[]{:S(2)}, u32[]{:S(2)}) async-start(f32[32,4,384]{2,1,0:T(4,128)} %shard_map.61), calls=%async_computation.1 | async-start | bytes 393216 | tf_op jit(solution)/shard_map/all_to_all | solution.py:889
  47.8 0.0 collective-permute-done.8
  47.8 1.7 %collective-permute-start.9 = (bf16[2,256,256]{2,1,0:T(8,128)(2,1)}, bf16[2,256,256]{2,1,0:T(8,128)(2,1)S(1)}, u32[]{:S(2)}, u32[]{:S(2)}) collective-permute-start(bf16[2,256,256]{2,1,0:T(8,128)(2,1)} %collective-permute-done.8), channel_id=1, source_target_pairs={{0,1},{1,0},{2,3},{3,2},{4,5},{5,4},{6,7},{7,6},{8,9},{9,8},{10,11... | collective-permute-start | bytes 786440 | tf_op jit(solution)/shard_map/ppermute | solution.py:811
  49.5 0.0 collective-permute-done.7.refs_1_
  49.5 1.5 %collective-permute-start.10 = (bf16[2,256,256]{2,1,0:T(8,128)(2,1)S(1)}, bf16[2,256,256]{2,1,0:T(8,128)(2,1)S(1)}, u32[]{:S(2)}, u32[]{:S(2)}) collective-permute-start(bf16[2,256,256]{2,1,0:T(8,128)(2,1)S(1)} %collective-permute-done.7.refs_1_), channel_id=1, source_target_pairs={{0,2},{1,7},{2,4},{3,1},{4,6},{5,3},{6,0},{7,5},{8,10},{9,15},{10,... | collective-permute-start | bytes 786440 | tf_op jit(solution)/shard_map/ppermute | solution.py:860
  51.0 0.0 collective-permute-done.6.refs_0_
  51.0 0.0 collective-permute-start.15
  51.0 0.0 collective-permute-done.14.refs_9_
  51.0 0.5 collective-permute-start.16
  51.6 0.0 collective-permute-done.13.refs_7_
  51.6 1.5 %collective-permute-start.17 = (bf16[2,256,256]{2,1,0:T(8,128)(2,1)S(1)}, bf16[2,256,256]{2,1,0:T(8,128)(2,1)S(1)}, u32[]{:S(2)}, u32[]{:S(2)}) collective-permute-start(bf16[2,256,256]{2,1,0:T(8,128)(2,1)S(1)} %collective-permute-done.close), channel_id=1, source_target_pairs={{0,2},{1,7},{2,4},{3,1},{4,6},{5,3},{6,0},{7,5},{8,10},{9,15},{10,... | collective-permute-start | bytes 786440 | tf_op jit(solution)/shard_map/ppermute | solution.py:874
  53.1 5.3 %collective-permute-done.9.refs_2_ = bf16[2,256,256]{2,1,0:T(8,128)(2,1)S(1)} collective-permute-done((bf16[2,256,256]{2,1,0:T(8,128)(2,1)}, bf16[2,256,256]{2,1,0:T(8,128)(2,1)S(1)}, u32[]{:S(2)}, u32[]{:S(2)}) %collective-permute-start.9) | collective-permute-done | bytes 262176 | tf_op jit(solution)/shard_map/ppermute | solution.py:811
  58.4 3.4 %collective-permute-done.10.refs_3_ = bf16[2,256,256]{2,1,0:T(8,128)(2,1)S(1)} collective-permute-done((bf16[2,256,256]{2,1,0:T(8,128)(2,1)S(1)}, bf16[2,256,256]{2,1,0:T(8,128)(2,1)S(1)}, u32[]{:S(2)}, u32[]{:S(2)}) %collective-permute-start.10) | collective-permute-done | bytes 262176 | tf_op jit(solution)/shard_map/ppermute | solution.py:860
  61.8 0.0 collective-permute-done.15.refs_10_
  61.8 0.0 collective-permute-done.16.refs_11_
  61.8 0.0 copy-done.1
  61.8 0.0 copy-done.4
  61.8 0.0 copy-done.5
  61.8 4.2 %shard_map.63 = (bf16[2,3,256,256]{3,2,1,0:T(8,128)(2,1)}, f32[2,256,256]{2,1,0:T(8,128)S(1)}, f32[256,256]{1,0:T(8,128)S(1)}) custom-call(s32[1]{0:T(128)} %bitcast.1.index.spot, s32[1]{0:T(128)} %bitcast.4.signs, f32[2,3]{1,0:T(2,128)S(1)} %copy-done.5, bf16[2,3,256,256]{3,2,1,0:T(8,128)(2,1)S(1)} %bitcast.10, ...), custom_call_target="tpu_custom_call" | custom-call | flops 26214400 | bytes 7602176 | tf_op jit(solution)/shard_map/pallas_call | solution.py:284
  66.0 0.8 %collective-permute-done.17.remote = bf16[2,256,256]{2,1,0:T(8,128)(2,1)S(1)} collective-permute-done((bf16[2,256,256]{2,1,0:T(8,128)(2,1)S(1)}, bf16[2,256,256]{2,1,0:T(8,128)(2,1)S(1)}, u32[]{:S(2)}, u32[]{:S(2)}) %collective-permute-start.17) | collective-permute-done | bytes 262176 | tf_op jit(solution)/shard_map/ppermute | solution.py:874
  66.9 0.8 %shard_map.64 = bf16[2,3,256,256]{3,2,1,0:T(8,128)(2,1)} custom-call(f32[2,256,256]{2,1,0:T(8,128)S(1)} %get-tuple-element.26.partial, f32[256,256]{1,0:T(8,128)S(1)} %get-tuple-element.27.speed, bf16[2,256,256]{2,1,0:T(8,128)(2,1)S(1)} %collective-permute-done.close, ...), custom_call_target="tpu_custom_call", output_to_operand_aliasing={{}: (4, {})} | custom-call | flops 524288 | bytes 3145728 | tf_op jit(solution)/shard_map/pallas_call | solution.py:284
  67.7 0.0 all-to-all-done.1.source
  67.7 1.0 %shard_map.62 = f32[3,1,64,256]{3,2,1,0:T(8,128)} custom-call(f32[32,4,384]{2,1,0:T(4,128)S(1)} %all-to-all-done.1.source, bf16[4,256,256]{2,1,0:T(8,128)(2,1)S(1)} %copy-done), custom_call_target="tpu_custom_call" | custom-call | bytes 1114112 | tf_op jit(solution)/shard_map/pallas_call | solution.py:284
Async XLA Ops:
  0.6 17.0 %copy-start = (bf16[4,256,256]{2,1,0:T(8,128)(2,1)S(1)}, bf16[4,256,256]{2,1,0:T(8,128)(2,1)}, u32[]{:S(2)}) copy-start(bf16[4,256,256]{2,1,0:T(8,128)(2,1)} %constant.16.clone.refs_7_.tables) | copy-start | bytes 1572868
  0.6 8.5 %collective-permute-start.4 = (f32[3,64,256]{2,1,0:T(8,128)}, f32[3,64,256]{2,1,0:T(8,128)S(1)}, u32[]{:S(2)}, u32[]{:S(2)}) collective-permute-start(f32[3,64,256]{2,1,0:T(8,128)} %bitcast.11), channel_id=1, source_target_pairs={{0,1},{1,0},{2,3},{3,2},{4,5},{5,4},{6,7},{7,6},{8,9},{9,8},{10,11... | collective-permute-start | bytes 589832 | tf_op jit(solution)/shard_map/ppermute | solution.py:811
  3.7 13.9 %copy-start.2 = (f32[3,1,64,256]{3,2,1,0:T(8,128)S(1)}, f32[3,1,64,256]{3,2,1,0:T(8,128)}, u32[]{:S(2)}) copy-start(f32[3,1,64,256]{3,2,1,0:T(8,128)} %param.4) | copy-start | bytes 589828
  6.1 7.2 %collective-permute-start.1 = (bf16[416,256]{1,0:T(8,128)(2,1)}, bf16[416,256]{1,0:T(8,128)(2,1)S(1)}, u32[]{:S(2)}, u32[]{:S(2)}) collective-permute-start(bf16[416,256]{1,0:T(8,128)(2,1)} %get-tuple-element.18), channel_id=1, source_target_pairs={{0,8},{8,16},{16,24},{24,0},{1,9},{9,17},{17,25},{25,1},{2,10},{10... | collective-permute-start | bytes 638984 | tf_op jit(solution)/shard_map/ppermute | solution.py:806
  6.2 8.4 %collective-permute-start.2 = (bf16[416,256]{1,0:T(8,128)(2,1)}, bf16[416,256]{1,0:T(8,128)(2,1)S(1)}, u32[]{:S(2)}, u32[]{:S(2)}) collective-permute-start(bf16[416,256]{1,0:T(8,128)(2,1)} %get-tuple-element.19), channel_id=1, source_target_pairs={{0,16},{8,24},{16,0},{24,8},{1,17},{9,25},{17,1},{25,9},{2,18},{10... | collective-permute-start | bytes 638984 | tf_op jit(solution)/shard_map/ppermute | solution.py:806
  7.7 9.9 %collective-permute-start.3 = (bf16[416,256]{1,0:T(8,128)(2,1)}, bf16[416,256]{1,0:T(8,128)(2,1)S(1)}, u32[]{:S(2)}, u32[]{:S(2)}) collective-permute-start(bf16[416,256]{1,0:T(8,128)(2,1)} %get-tuple-element.20), channel_id=1, source_target_pairs={{0,24},{8,0},{16,8},{24,16},{1,25},{9,1},{17,9},{25,17},{2,26},{10... | collective-permute-start | bytes 638984 | tf_op jit(solution)/shard_map/ppermute | solution.py:806
  9.1 8.5 %collective-permute-start.5 = (f32[3,64,256]{2,1,0:T(8,128)S(1)}, f32[3,64,256]{2,1,0:T(8,128)S(1)}, u32[]{:S(2)}, u32[]{:S(2)}) collective-permute-start(f32[3,64,256]{2,1,0:T(8,128)S(1)} %collective-permute-done.4.refs_5_), channel_id=1, source_target_pairs={{0,2},{1,7},{2,4},{3,1},{4,6},{5,3},{6,0},{7,5},{8,10},{9,15},{10,... | collective-permute-start | bytes 589832 | tf_op jit(solution)/shard_map/ppermute | solution.py:853
  19.2 24.3 %all-to-all-start = ((f32[32,8,384]{2,1,0:T(8,128)}), f32[32,8,384]{2,1,0:T(8,128)S(1)}, u32[]{:S(2)}, u32[]{:S(2)}) async-start(f32[32,8,384]{2,1,0:T(8,128)} %bitcast.5), calls=%async_computation | async-start | bytes 786432 | tf_op jit(solution)/shard_map/all_to_all | solution.py:866
  24.4 37.4 %copy-start.1 = (bf16[2,3,1,256,256]{4,3,2,1,0:T(8,128)(2,1)S(1)}, bf16[2,3,1,256,256]{4,3,2,1,0:T(8,128)(2,1)}, u32[]{:S(2)}) copy-start(bf16[2,3,1,256,256]{4,3,2,1,0:T(8,128)(2,1)} %param.5) | copy-start | bytes 2359300
  24.4 10.6 %collective-permute-start.11 = (f32[3,64,256]{2,1,0:T(8,128)S(1)}, f32[3,64,256]{2,1,0:T(8,128)S(1)}, u32[]{:S(2)}, u32[]{:S(2)}) collective-permute-start(f32[3,64,256]{2,1,0:T(8,128)S(1)} %bitcast.14), channel_id=1, source_target_pairs={{0,16},{8,24},{16,0},{24,8},{1,17},{9,25},{17,1},{25,9},{2,18},{10... | collective-permute-start | bytes 589832 | tf_op jit(solution)/shard_map/ppermute | solution.py:811
  26.3 10.2 %collective-permute-start.12 = (f32[3,64,256]{2,1,0:T(8,128)S(1)}, f32[3,64,256]{2,1,0:T(8,128)S(1)}, u32[]{:S(2)}, u32[]{:S(2)}) collective-permute-start(f32[3,64,256]{2,1,0:T(8,128)S(1)} %bitcast.15), channel_id=1, source_target_pairs={{0,8},{8,0},{16,24},{24,16},{1,9},{9,1},{17,25},{25,17},{2,10},{10... | collective-permute-start | bytes 589832 | tf_op jit(solution)/shard_map/ppermute | solution.py:811
  26.3 11.6 %collective-permute-start = (bf16[2,256,256]{2,1,0:T(8,128)(2,1)}, bf16[2,256,256]{2,1,0:T(8,128)(2,1)S(1)}, u32[]{:S(2)}, u32[]{:S(2)}) collective-permute-start(bf16[2,256,256]{2,1,0:T(8,128)(2,1)} %get-tuple-element.16), channel_id=1, source_target_pairs={{0,1},{1,0},{2,3},{3,2},{4,5},{5,4},{6,7},{7,6},{8,9},{9,8},{10,11... | collective-permute-start | bytes 786440 | tf_op jit(solution)/shard_map/ppermute | solution.py:811
  27.7 20.0 %collective-permute-start.8 = (bf16[2,256,256]{2,1,0:T(8,128)(2,1)}, bf16[2,256,256]{2,1,0:T(8,128)(2,1)}, u32[]{:S(2)}, u32[]{:S(2)}) collective-permute-start(bf16[2,256,256]{2,1,0:T(8,128)(2,1)} %get-tuple-element.23), channel_id=1, source_target_pairs={{2,0},{7,1},{4,2},{1,3},{6,4},{3,5},{0,6},{5,7},{10,8},{15,9},{12,... | collective-permute-start | bytes 786440 | tf_op jit(solution)/shard_map/ppermute | solution.py:858
  31.1 18.4 %collective-permute-start.7 = (bf16[2,256,256]{2,1,0:T(8,128)(2,1)}, bf16[2,256,256]{2,1,0:T(8,128)(2,1)S(1)}, u32[]{:S(2)}, u32[]{:S(2)}) collective-permute-start(bf16[2,256,256]{2,1,0:T(8,128)(2,1)} %get-tuple-element.24), channel_id=1, source_target_pairs={{0,1},{1,0},{2,3},{3,2},{4,5},{5,4},{6,7},{7,6},{8,9},{9,8},{10,11... | collective-permute-start | bytes 786440 | tf_op jit(solution)/shard_map/ppermute | solution.py:811
  35.0 16.0 %collective-permute-start.6 = (bf16[2,256,256]{2,1,0:T(8,128)(2,1)}, bf16[2,256,256]{2,1,0:T(8,128)(2,1)S(1)}, u32[]{:S(2)}, u32[]{:S(2)}) collective-permute-start(bf16[2,256,256]{2,1,0:T(8,128)(2,1)} %get-tuple-element.23), channel_id=1, source_target_pairs={{0,1},{1,0},{2,3},{3,2},{4,5},{5,4},{6,7},{7,6},{8,9},{9,8},{10,11... | collective-permute-start | bytes 786440 | tf_op jit(solution)/shard_map/ppermute | solution.py:811
  36.5 0.7 copy-start.3
  37.2 13.9 %collective-permute-start.14 = (f32[4,64,256]{2,1,0:T(8,128)S(1)}, f32[4,64,256]{2,1,0:T(8,128)S(1)}, u32[]{:S(2)}, u32[]{:S(2)}) collective-permute-start(f32[4,64,256]{2,1,0:T(8,128)S(1)} %get-tuple-element.25.refs_8_), channel_id=1, source_target_pairs={{0,16},{8,24},{16,0},{24,8},{1,17},{9,25},{17,1},{25,9},{2,18},{10... | collective-permute-start | bytes 786440 | tf_op jit(solution)/shard_map/ppermute | solution.py:811
  37.9 13.7 %collective-permute-start.13 = (f32[3,64,256]{2,1,0:T(8,128)S(1)}, f32[3,64,256]{2,1,0:T(8,128)}, u32[]{:S(2)}, u32[]{:S(2)}) collective-permute-start(f32[3,64,256]{2,1,0:T(8,128)S(1)} %collective-permute-done.11.refs_5_), channel_id=1, source_target_pairs={{0,8},{8,0},{16,24},{24,16},{1,9},{9,1},{17,25},{25,17},{2,10},{10... | collective-permute-start | bytes 589832 | tf_op jit(solution)/shard_map/ppermute | solution.py:811
  45.0 16.8 %copy-start.4 = (f32[3,64,256]{2,1,0:T(8,128)S(1)}, f32[3,64,256]{2,1,0:T(8,128)}, u32[]{:S(2)}) copy-start(f32[3,64,256]{2,1,0:T(8,128)} %copy-done.3) | copy-start | bytes 589828
  45.0 16.8 %copy-start.5 = (f32[2,3]{1,0:T(2,128)S(1)}, f32[2,3]{1,0:T(2,128)}, u32[]{:S(2)}) copy-start(f32[2,3]{1,0:T(2,128)} %kick.1) | copy-start | bytes 76
  45.1 22.7 %all-to-all-start.1 = ((f32[32,4,384]{2,1,0:T(4,128)}), f32[32,4,384]{2,1,0:T(4,128)S(1)}, u32[]{:S(2)}, u32[]{:S(2)}) async-start(f32[32,4,384]{2,1,0:T(4,128)} %shard_map.61), calls=%async_computation.1 | async-start | bytes 393216 | tf_op jit(solution)/shard_map/all_to_all | solution.py:889
  47.8 10.6 %collective-permute-start.9 = (bf16[2,256,256]{2,1,0:T(8,128)(2,1)}, bf16[2,256,256]{2,1,0:T(8,128)(2,1)S(1)}, u32[]{:S(2)}, u32[]{:S(2)}) collective-permute-start(bf16[2,256,256]{2,1,0:T(8,128)(2,1)} %collective-permute-done.8), channel_id=1, source_target_pairs={{0,1},{1,0},{2,3},{3,2},{4,5},{5,4},{6,7},{7,6},{8,9},{9,8},{10,11... | collective-permute-start | bytes 786440 | tf_op jit(solution)/shard_map/ppermute | solution.py:811
  49.5 12.3 %collective-permute-start.10 = (bf16[2,256,256]{2,1,0:T(8,128)(2,1)S(1)}, bf16[2,256,256]{2,1,0:T(8,128)(2,1)S(1)}, u32[]{:S(2)}, u32[]{:S(2)}) collective-permute-start(bf16[2,256,256]{2,1,0:T(8,128)(2,1)S(1)} %collective-permute-done.7.refs_1_), channel_id=1, source_target_pairs={{0,2},{1,7},{2,4},{3,1},{4,6},{5,3},{6,0},{7,5},{8,10},{9,15},{10,... | collective-permute-start | bytes 786440 | tf_op jit(solution)/shard_map/ppermute | solution.py:860
  51.0 10.8 %collective-permute-start.15 = (f32[4,64,256]{2,1,0:T(8,128)S(1)}, f32[4,64,256]{2,1,0:T(8,128)S(1)}, u32[]{:S(2)}, u32[]{:S(2)}) collective-permute-start(f32[4,64,256]{2,1,0:T(8,128)S(1)} %get-tuple-element.25.refs_8_), channel_id=1, source_target_pairs={{0,8},{8,0},{16,24},{24,16},{1,9},{9,1},{17,25},{25,17},{2,10},{10... | collective-permute-start | bytes 786440 | tf_op jit(solution)/shard_map/ppermute | solution.py:811
  51.0 10.8 %collective-permute-start.16 = (f32[4,64,256]{2,1,0:T(8,128)S(1)}, f32[4,64,256]{2,1,0:T(8,128)S(1)}, u32[]{:S(2)}, u32[]{:S(2)}) collective-permute-start(f32[4,64,256]{2,1,0:T(8,128)S(1)} %collective-permute-done.14.refs_9_), channel_id=1, source_target_pairs={{0,8},{8,0},{16,24},{24,16},{1,9},{9,1},{17,25},{25,17},{2,10},{10... | collective-permute-start | bytes 786440 | tf_op jit(solution)/shard_map/ppermute | solution.py:811
  51.6 15.3 %collective-permute-start.17 = (bf16[2,256,256]{2,1,0:T(8,128)(2,1)S(1)}, bf16[2,256,256]{2,1,0:T(8,128)(2,1)S(1)}, u32[]{:S(2)}, u32[]{:S(2)}) collective-permute-start(bf16[2,256,256]{2,1,0:T(8,128)(2,1)S(1)} %collective-permute-done.close), channel_id=1, source_target_pairs={{0,2},{1,7},{2,4},{3,1},{4,6},{5,3},{6,0},{7,5},{8,10},{9,15},{10,... | collective-permute-start | bytes 786440 | tf_op jit(solution)/shard_map/ppermute | solution.py:874
